TPU v7x, 32 devices: a whole 2x2x4 slice. The times are simulated.
32 devices in a mesh: leaf: 16 (over z, y, x), sep: 2 (over core).
Axes of the slice: x: 2, y: 2, z: 4, core: 2. Of those that a mesh axis runs over, the one named last changes fastest.
Arguments:
- leaf_rhs: bfloat16 [16, 256, 2048], P('leaf', None, 'sep'), may hold values from -6 to 6
- leaf_inv: bfloat16 [16, 2048, 2048], P('leaf', 'sep'), may hold values from -0.125 to 0.125
- leaf_couple: bfloat16 [16, 512, 2048], P('leaf', None, 'sep'), may hold values from -0.0625 to 0.0625
- sep_rhs: float32 [16, 256, 512], P('leaf', None, 'sep'), may hold values from -6 to 6
- sep_inv: float32 [16, 512, 512], P('leaf', 'sep'), may hold values from -0.25 to 0.25
- sep_couple: float32 [16, 512, 512], P('leaf', None, 'sep'), may hold values from -0.1875 to 0.1875
Outputs:
- leaf_solution: float32 [16, 256, 2048], P('leaf', None, 'sep')
- sep_solution: float32 [16, 256, 512], P('leaf', None, 'sep')
All inputs are finite; a program needn't handle non-finite values.
Results may differ from a plain program's by a relative error of at most 0.0042.
Values may be sent and summed in bfloat16 or wider, within the bound.
No kernel may reach another device: no remote copies, remote signals or barrier semaphores. Data moves between devices by JAX's collectives and lax.ppermute only.
A program may use at most 128 MiB of HBM per device.

v0:
```python
import jax
import jax.numpy as jnp
from jax import lax
from jax.sharding import PartitionSpec as P


def partner(value, axis, apart):
    mask = 2**apart
    pairs = [(source, source ^ mask) for source in range(lax.axis_size(axis))]
    return lax.ppermute(value, axis, pairs)


def times_transposed(left, right):
    return lax.dot_general(
        left,
        right,
        (((1,), (1,)), ((), ())),
        precision=lax.Precision.HIGHEST,
        preferred_element_type=jnp.float32,
    )


def times_plain(left, right):
    return jnp.dot(left, right, precision=lax.Precision.HIGHEST, preferred_element_type=jnp.float32)


def device_level(place, depth):
    level = jnp.int32(1)
    running = jnp.bool_(True)
    for bit in range(depth + 1):
        running = running & (place >> bit & 1 == 1)
        level = level + running.astype(jnp.int32)
    return level


def local(leaf_rhs, leaf_inv, leaf_couple, sep_rhs, sep_inv, sep_couple):
    depth = lax.axis_size("leaf").bit_length() - 1
    place = lax.axis_index("leaf")
    level = device_level(place, depth)
    rhs_local = leaf_rhs[0]
    inv_rows = leaf_inv[0]
    couple_cols = leaf_couple[0]
    sep_local = sep_rhs[0]
    sep_rows = sep_inv[0]
    sep_cols = sep_couple[0]
    rows = rhs_local.shape[0]
    half_sep = sep_rows.shape[0]
    width = sep_rows.shape[1]
    leaf_forward = lax.dot_general(
        lax.all_gather(rhs_local, "sep", axis=1, tiled=True),
        inv_rows,
        (((1,), (1,)), ((), ())),
        preferred_element_type=jnp.float32,
    )
    leaf_state = leaf_forward.astype(jnp.bfloat16)
    outgoing = lax.dot_general(
        leaf_state, couple_cols, (((1,), (1,)), ((), ())), preferred_element_type=jnp.float32
    )
    carry_rhs, carry_inv, carry_cols = (sep_local, sep_rows, sep_cols)
    ancestry = []
    for bit in range(depth):
        other_rhs, other_inv, other_cols = partner((carry_rhs, carry_inv, carry_cols), "leaf", bit)
        is_upper = place >> bit & 1 == 1
        ancestry.append(
            (
                jnp.where(is_upper, other_rhs, carry_rhs),
                jnp.where(is_upper, other_inv, carry_inv),
                jnp.where(is_upper, other_cols, carry_cols),
            )
        )
        carry_rhs = jnp.where(is_upper, carry_rhs, other_rhs)
        carry_inv = jnp.where(is_upper, carry_inv, other_inv)
        carry_cols = jnp.where(is_upper, carry_cols, other_cols)
    ancestry.append((carry_rhs, carry_inv, carry_cols))
    states = []
    mine = outgoing
    for section in range(1, depth + 2):
        rhs_half, inv_part, cols_part = ancestry[section - 1]
        share = lax.psum_scatter(mine, "sep", scatter_dimension=1, tiled=True)
        total = share
        if section <= depth:
            total = share + partner(share, "leaf", section - 1)
        whole_work = lax.all_gather(rhs_half - total, "sep", axis=1, tiled=True)
        fresh = times_transposed(whole_work, inv_part)
        states.append(fresh)
        if section <= depth:
            mine = times_transposed(fresh, cols_part)
    sep_solution = jnp.zeros((rows, half_sep), jnp.float32)
    parent_full = jnp.zeros((rows, width), jnp.float32)
    for section in range(depth + 1, 0, -1):
        rhs_half, inv_part, cols_part = ancestry[section - 1]
        if section == depth + 1:
            work = states[section - 1]
        else:
            work = states[section - 1] - times_plain(parent_full, cols_part)
        partial_value = times_plain(work, inv_part)
        current = lax.psum_scatter(partial_value, "sep", scatter_dimension=1, tiled=True)
        sep_solution = jnp.where(level == section, current, sep_solution)
        parent_full = lax.all_gather(current, "sep", axis=1, tiled=True)
    pulled = jnp.dot(
        parent_full.astype(jnp.bfloat16), couple_cols, preferred_element_type=jnp.float32
    )
    residue = (leaf_state.astype(jnp.float32) - pulled).astype(jnp.bfloat16)
    spread = jnp.dot(residue, inv_rows, preferred_element_type=jnp.float32)
    leaf_solution = lax.psum_scatter(spread, "sep", scatter_dimension=1, tiled=True)
    return (leaf_solution[None], sep_solution[None])


def solution(mesh):
    return jax.shard_map(
        local,
        mesh=mesh,
        in_specs=(
            P("leaf", None, "sep"),
            P("leaf", "sep", None),
            P("leaf", None, "sep"),
            P("leaf", None, "sep"),
            P("leaf", "sep", None),
            P("leaf", None, "sep"),
        ),
        out_specs=(P("leaf", None, "sep"), P("leaf", None, "sep")),
        check_vma=False,
    )
```

profile of v0, /device:TPU:0, one launch (start us, length us, event | category | flops | bytes accessed | tf_op | source)
XLA Modules:
  0.0 328.7 jit_solution(13412599410338617865)
XLA Ops:
  8.0 13.3 %all-gather.3.cloned.1.call-done = bf16[1,256,2048]{2,1,0:T(8,128)(2,1)} async-done(((bf16[1,256,1024]{2,1,0:T(8,128)(2,1)}), bf16[1,256,2048]{2,1,0:T(8,128)(2,1)}) %all-gather.3.cloned.1.call-update) | async-done | bytes 1048592 | tf_op jit(solution)/shard_map/all_gather | solution.py:50
  21.3 3.8 %fusion.5 = bf16[256,1024]{1,0:T(8,128)(2,1)S(1)} fusion(bf16[1,1024,2048]{2,1,0:T(8,128)(2,1)} %param.7, bf16[1,256,2048]{2,1,0:T(8,128)(2,1)} %all-gather.3.cloned.1.call-done), kind=kOutput, calls=%fused_computation.6 | convolution fusion | flops 1074003968 | bytes 5767168 | tf_op jit(solution)/shard_map/dot_general | solution.py:49
  27.3 1.8 collective-permute-start
  29.1 7.4 %reduce-scatter.12.cloned.1.call-done = f32[256,256]{1,0:T(8,128)} async-done(((f32[256,512]{1,0:T(8,128)}), f32[256,256]{1,0:T(8,128)}) %reduce-scatter.12.cloned.1.call-update) | async-done | bytes 262160 | tf_op jit(solution)/shard_map/reduce_scatter | solution.py:79
  40.2 5.8 %collective-permute-done.1 = f32[256,256]{1,0:T(8,128)} collective-permute-done((f32[256,256]{1,0:T(8,128)}, f32[256,256]{1,0:T(8,128)}, u32[]{:S(2)}, u32[]{:S(2)}) %collective-permute-start.1) | collective-permute-done | bytes 262176 | tf_op jit(solution)/shard_map/ppermute | solution.py:10
  46.0 1.9 broadcast_select_fusion.35
  47.9 2.2 all_gather.34
  50.1 7.1 %collective-permute-done.2 = f32[256,512]{1,0:T(8,128)S(1)} collective-permute-done((f32[256,512]{1,0:T(8,128)S(1)}, f32[256,512]{1,0:T(8,128)S(1)}, u32[]{:S(2)}, u32[]{:S(2)}) %collective-permute-start.2) | collective-permute-done | bytes 524320 | tf_op jit(solution)/shard_map/ppermute | solution.py:10
  57.8 9.9 %collective-permute-done.4 = f32[512,256]{1,0:T(8,128)S(1)} collective-permute-done((f32[512,256]{1,0:T(8,128)S(1)}, f32[512,256]{1,0:T(8,128)S(1)}, u32[]{:S(2)}, u32[]{:S(2)}) %collective-permute-start.4) | collective-permute-done | bytes 524320 | tf_op jit(solution)/shard_map/ppermute | solution.py:10
  70.4 1.8 collective-permute-start.6
  72.5 6.0 %reduce-scatter.14.cloned.1.call-done = f32[256,256]{1,0:T(8,128)} async-done(((f32[256,512]{1,0:T(8,128)}), f32[256,256]{1,0:T(8,128)}) %reduce-scatter.14.cloned.1.call-update) | async-done | bytes 262160 | tf_op jit(solution)/shard_map/reduce_scatter | solution.py:79
  80.6 10.4 %collective-permute-done.3 = f32[256,256]{1,0:T(8,128)} collective-permute-done((f32[256,256]{1,0:T(8,128)}, f32[256,256]{1,0:T(8,128)}, u32[]{:S(2)}, u32[]{:S(2)}) %collective-permute-start.3) | collective-permute-done | bytes 262176 | tf_op jit(solution)/shard_map/ppermute | solution.py:10
  90.9 5.5 %collective-permute-done.5 = f32[256,256]{1,0:T(8,128)S(1)} collective-permute-done((f32[256,256]{1,0:T(8,128)}, f32[256,256]{1,0:T(8,128)S(1)}, u32[]{:S(2)}, u32[]{:S(2)}) %collective-permute-start.5) | collective-permute-done | bytes 262176 | tf_op jit(solution)/shard_map/ppermute | solution.py:10
  96.5 1.9 broadcast_select_fusion.34
  98.3 2.2 all_gather.35
  101.2 5.1 %collective-permute-done.8 = f32[512,256]{1,0:T(8,128)S(1)} collective-permute-done((f32[512,256]{1,0:T(8,128)S(1)}, f32[512,256]{1,0:T(8,128)S(1)}, u32[]{:S(2)}, u32[]{:S(2)}) %collective-permute-start.8) | collective-permute-done | bytes 524320 | tf_op jit(solution)/shard_map/ppermute | solution.py:10
  108.9 1.8 collective-permute-start.10
  111.0 5.1 %reduce-scatter.16.cloned.1.call-done = f32[256,256]{1,0:T(8,128)} async-done(((f32[256,512]{1,0:T(8,128)}), f32[256,256]{1,0:T(8,128)}) %reduce-scatter.16.cloned.1.call-update) | async-done | bytes 262160 | tf_op jit(solution)/shard_map/reduce_scatter | solution.py:79
  116.0 1.7 collective-permute-start.9
  119.2 10.2 %collective-permute-done.7 = f32[256,256]{1,0:T(8,128)} collective-permute-done((f32[256,256]{1,0:T(8,128)}, f32[256,256]{1,0:T(8,128)}, u32[]{:S(2)}, u32[]{:S(2)}) %collective-permute-start.7) | collective-permute-done | bytes 262176 | tf_op jit(solution)/shard_map/ppermute | solution.py:10
  129.5 5.5 %collective-permute-done.9 = f32[256,256]{1,0:T(8,128)S(1)} collective-permute-done((f32[256,256]{1,0:T(8,128)}, f32[256,256]{1,0:T(8,128)S(1)}, u32[]{:S(2)}, u32[]{:S(2)}) %collective-permute-start.9) | collective-permute-done | bytes 262176 | tf_op jit(solution)/shard_map/ppermute | solution.py:10
  135.0 1.9 broadcast_select_fusion.33
  136.9 2.2 all_gather.36
  139.7 4.2 %collective-permute-done.12 = f32[512,256]{1,0:T(8,128)S(1)} collective-permute-done((f32[512,256]{1,0:T(8,128)S(1)}, f32[512,256]{1,0:T(8,128)S(1)}, u32[]{:S(2)}, u32[]{:S(2)}) %collective-permute-start.12) | collective-permute-done | bytes 524320 | tf_op jit(solution)/shard_map/ppermute | solution.py:10
  147.4 2.7 collective-permute-start.14
  150.3 3.2 reduce-scatter.18.cloned.1.call-done
  153.6 2.6 collective-permute-start.13
  157.7 42.9 %collective-permute-done.11 = f32[256,256]{1,0:T(8,128)} collective-permute-done((f32[256,256]{1,0:T(8,128)}, f32[256,256]{1,0:T(8,128)}, u32[]{:S(2)}, u32[]{:S(2)}) %collective-permute-start.11) | collective-permute-done | bytes 262176 | tf_op jit(solution)/shard_map/ppermute | solution.py:10
  200.6 5.5 %collective-permute-done.13 = f32[256,256]{1,0:T(8,128)S(1)} collective-permute-done((f32[256,256]{1,0:T(8,128)}, f32[256,256]{1,0:T(8,128)S(1)}, u32[]{:S(2)}, u32[]{:S(2)}) %collective-permute-start.13) | collective-permute-done | bytes 262176 | tf_op jit(solution)/shard_map/ppermute | solution.py:10
  207.2 2.2 all_gather.37
  210.1 6.1 %collective-permute-done.15 = f32[512,256]{1,0:T(8,128)S(1)} collective-permute-done((f32[512,256]{1,0:T(8,128)S(1)}, f32[512,256]{1,0:T(8,128)S(1)}, u32[]{:S(2)}, u32[]{:S(2)}) %collective-permute-start.15) | collective-permute-done | bytes 524320 | tf_op jit(solution)/shard_map/ppermute | solution.py:10
  218.5 7.3 %reduce-scatter.20.cloned.1.call-done = f32[256,256]{1,0:T(8,128)} async-done(((f32[256,512]{1,0:T(8,128)}), f32[256,256]{1,0:T(8,128)}) %reduce-scatter.20.cloned.1.call-update) | async-done | bytes 262160 | tf_op jit(solution)/shard_map/reduce_scatter | solution.py:79
  226.9 2.2 all_gather.38
  230.8 2.5 fusion.27
  233.3 7.3 %reduce-scatter.22.cloned.1.call-done = f32[256,256]{1,0:T(8,128)} async-done(((f32[256,512]{1,0:T(8,128)}), f32[256,256]{1,0:T(8,128)}) %reduce-scatter.22.cloned.1.call-update) | async-done | bytes 262160 | tf_op jit(solution)/shard_map/reduce_scatter | solution.py:97
  240.6 2.6 all_gather.39
  243.2 1.7 convolution_subtract_fusion.4
  246.4 10.2 %reduce-scatter.24.cloned.1.call-done = f32[256,256]{1,0:T(8,128)} async-done(((f32[256,512]{1,0:T(8,128)}), f32[256,256]{1,0:T(8,128)}) %reduce-scatter.24.cloned.1.call-update) | async-done | bytes 262160 | tf_op jit(solution)/shard_map/reduce_scatter | solution.py:97
  256.6 2.4 all_gather.40
  260.6 2.6 fusion.22
  263.3 9.3 %reduce-scatter.26.cloned.1.call-done = f32[256,256]{1,0:T(8,128)} async-done(((f32[256,512]{1,0:T(8,128)}), f32[256,256]{1,0:T(8,128)}) %reduce-scatter.26.cloned.1.call-update) | async-done | bytes 262160 | tf_op jit(solution)/shard_map/reduce_scatter | solution.py:97
  272.5 2.4 all_gather.41
  278.0 10.4 %reduce-scatter.28.cloned.1.call-done = f32[256,256]{1,0:T(8,128)} async-done(((f32[256,512]{1,0:T(8,128)}), f32[256,256]{1,0:T(8,128)}) %reduce-scatter.28.cloned.1.call-update) | async-done | bytes 262160 | tf_op jit(solution)/shard_map/reduce_scatter | solution.py:97
  288.4 2.4 all_gather.42
  293.0 10.2 %reduce-scatter.30.cloned.1.call-done = f32[256,256]{1,0:T(8,128)} async-done(((f32[256,512]{1,0:T(8,128)}), f32[256,256]{1,0:T(8,128)}) %reduce-scatter.30.cloned.1.call-update) | async-done | bytes 262160 | tf_op jit(solution)/shard_map/reduce_scatter | solution.py:97
  303.2 2.4 all_gather.43
  305.6 5.3 %fusion = f32[256,2048]{1,0:T(8,128)} fusion(bf16[1,1024,2048]{2,1,0:T(8,128)(2,1)} %param.7, bf16[1,512,1024]{2,1,0:T(8,128)(2,1)S(1)} %copy-done, bf16[256,1024]{1,0:T(8,128)(2,1)} %copy-done.21, f32[256,512]{1,0:T(8,128)S(1)} %all_gather.43), kind=kOutput, calls=%fused_computation | convolution fusion | flops 1343094784 | bytes 8388608 | tf_op jit(solution)/shard_map/dot_general | solution.py:104
  311.8 10.0 %reduce-scatter.32.cloned.1.call-done = f32[256,1024]{1,0:T(8,128)} async-done(((f32[256,2048]{1,0:T(8,128)}), f32[256,1024]{1,0:T(8,128)}) %reduce-scatter.32.cloned.1.call-update) | async-done | bytes 1048592 | tf_op jit(solution)/shard_map/reduce_scatter | solution.py:105
  (109 shorter events, 39.3 us)
Async XLA Ops:
  7.2 18.7 %copy-start = (bf16[1,512,1024]{2,1,0:T(8,128)(2,1)S(1)}, bf16[1,512,1024]{2,1,0:T(8,128)(2,1)}, u32[]{:S(2)}) copy-start(bf16[1,512,1024]{2,1,0:T(8,128)(2,1)} %param.8) | copy-start | bytes 3145732
  7.2 14.1 %all-gather.3.cloned.1.call-start = ((), (), s32[]{:S(2)}) async-start(), calls=%async_computation.22 | async-start | bytes 1572864 | tf_op jit(solution)/shard_map/all_gather | solution.py:50
  7.9 19.4 %copy-start.22 = (f32[1,256,256]{2,1,0:T(8,128)S(1)}, f32[1,256,256]{2,1,0:T(8,128)}, u32[]{:S(2)}) copy-start(f32[1,256,256]{2,1,0:T(8,128)} %param.9) | copy-start | bytes 786436
  7.9 30.3 %copy-start.9 = (f32[1,256,512]{2,1,0:T(8,128)S(1)}, f32[1,256,512]{2,1,0:T(8,128)}, u32[]{:S(2)}) copy-start(f32[1,256,512]{2,1,0:T(8,128)} %param.10) | copy-start | bytes 1572868
  7.9 30.6 %copy-start.2 = (f32[1,512,256]{2,1,0:T(8,128)S(1)}, f32[1,512,256]{2,1,0:T(8,128)}, u32[]{:S(2)}) copy-start(f32[1,512,256]{2,1,0:T(8,128)} %param.11) | copy-start | bytes 1572868
  7.9 28.6 %reduce-scatter.12.cloned.1.call-start = ((), (), s32[]{:S(2)}) async-start(), calls=%async_computation.11 | async-start | bytes 786432 | tf_op jit(solution)/shard_map/reduce_scatter | solution.py:79
  27.3 51.2 %reduce-scatter.14.cloned.1.call-start = ((), (), s32[]{:S(2)}) async-start(), calls=%async_computation.12 | async-start | bytes 786432 | tf_op jit(solution)/shard_map/reduce_scatter | solution.py:79
  27.3 12.9 %collective-permute-start = (f32[256,256]{1,0:T(8,128)S(1)}, f32[256,256]{1,0:T(8,128)}, u32[]{:S(2)}, u32[]{:S(2)}) collective-permute-start(f32[256,256]{1,0:T(8,128)S(1)} %bitcast.64), channel_id=1, source_target_pairs={{0,2},{2,0},{4,6},{6,4},{8,10},{10,8},{12,14},{14,12},{16,18},{18,... | collective-permute-start | bytes 786440 | tf_op jit(solution)/shard_map/ppermute | solution.py:10
  36.5 9.5 %collective-permute-start.1 = (f32[256,256]{1,0:T(8,128)}, f32[256,256]{1,0:T(8,128)}, u32[]{:S(2)}, u32[]{:S(2)}) collective-permute-start(f32[256,256]{1,0:T(8,128)} %reduce-scatter.12.cloned.1.call-done), channel_id=1, source_target_pairs={{0,2},{2,0},{4,6},{6,4},{8,10},{10,8},{12,14},{14,12},{16,18},{18,... | collective-permute-start | bytes 786440 | tf_op jit(solution)/shard_map/ppermute | solution.py:10
  38.2 18.9 %collective-permute-start.2 = (f32[256,512]{1,0:T(8,128)S(1)}, f32[256,512]{1,0:T(8,128)S(1)}, u32[]{:S(2)}, u32[]{:S(2)}) collective-permute-start(f32[256,512]{1,0:T(8,128)S(1)} %bitcast.63), channel_id=1, source_target_pairs={{0,2},{2,0},{4,6},{6,4},{8,10},{10,8},{12,14},{14,12},{16,18},{18,... | collective-permute-start | bytes 1572872 | tf_op jit(solution)/shard_map/ppermute | solution.py:10
  38.5 29.1 %collective-permute-start.4 = (f32[512,256]{1,0:T(8,128)S(1)}, f32[512,256]{1,0:T(8,128)S(1)}, u32[]{:S(2)}, u32[]{:S(2)}) collective-permute-start(f32[512,256]{1,0:T(8,128)S(1)} %bitcast.62), channel_id=1, source_target_pairs={{0,2},{2,0},{4,6},{6,4},{8,10},{10,8},{12,14},{14,12},{16,18},{18,... | collective-permute-start | bytes 1572872 | tf_op jit(solution)/shard_map/ppermute | solution.py:10
  57.1 12.1 %copy-start.11 = (f32[256,512]{1,0:T(8,128)}, f32[256,512]{1,0:T(8,128)S(1)}, u32[]{:S(2)}) copy-start(f32[256,512]{1,0:T(8,128)S(1)} %collective-permute-done.2) | copy-start | bytes 1572868
  67.7 33.5 %copy-start.4 = (f32[512,256]{1,0:T(8,128)}, f32[512,256]{1,0:T(8,128)S(1)}, u32[]{:S(2)}) copy-start(f32[512,256]{1,0:T(8,128)S(1)} %collective-permute-done.4) | copy-start | bytes 1572868
  69.2 46.9 %reduce-scatter.16.cloned.1.call-start = ((), (), s32[]{:S(2)}) async-start(), calls=%async_computation.13 | async-start | bytes 786432 | tf_op jit(solution)/shard_map/reduce_scatter | solution.py:79
  70.4 30.1 %collective-permute-start.6 = (f32[256,512]{1,0:T(8,128)S(1)}, f32[256,512]{1,0:T(8,128)}, u32[]{:S(2)}, u32[]{:S(2)}) collective-permute-start(f32[256,512]{1,0:T(8,128)S(1)} %broadcast_select_fusion.13), channel_id=1, source_target_pairs={{0,4},{2,6},{4,0},{6,2},{8,12},{10,14},{12,8},{14,10},{16,20},{18,... | collective-permute-start | bytes 1572872 | tf_op jit(solution)/shard_map/ppermute | solution.py:10
  72.2 18.8 %collective-permute-start.3 = (f32[256,256]{1,0:T(8,128)}, f32[256,256]{1,0:T(8,128)}, u32[]{:S(2)}, u32[]{:S(2)}) collective-permute-start(f32[256,256]{1,0:T(8,128)} %get-tuple-element.6), channel_id=1, source_target_pairs={{0,4},{2,6},{4,0},{6,2},{8,12},{10,14},{12,8},{14,10},{16,20},{18,... | collective-permute-start | bytes 786440 | tf_op jit(solution)/shard_map/ppermute | solution.py:10
  78.4 18.0 %collective-permute-start.5 = (f32[256,256]{1,0:T(8,128)}, f32[256,256]{1,0:T(8,128)S(1)}, u32[]{:S(2)}, u32[]{:S(2)}) collective-permute-start(f32[256,256]{1,0:T(8,128)} %reduce-scatter.14.cloned.1.call-done), channel_id=1, source_target_pairs={{0,4},{2,6},{4,0},{6,2},{8,12},{10,14},{12,8},{14,10},{16,20},{18,... | collective-permute-start | bytes 786440 | tf_op jit(solution)/shard_map/ppermute | solution.py:10
  80.2 26.0 %collective-permute-start.8 = (f32[512,256]{1,0:T(8,128)S(1)}, f32[512,256]{1,0:T(8,128)S(1)}, u32[]{:S(2)}, u32[]{:S(2)}) collective-permute-start(f32[512,256]{1,0:T(8,128)S(1)} %broadcast_select_fusion.11), channel_id=1, source_target_pairs={{0,4},{2,6},{4,0},{6,2},{8,12},{10,14},{12,8},{14,10},{16,20},{18,... | collective-permute-start | bytes 1572872 | tf_op jit(solution)/shard_map/ppermute | solution.py:10
  101.2 5.1 %copy-start.12 = (f32[256,256]{1,0:T(8,128)}, f32[256,256]{1,0:T(8,128)S(1)}, u32[]{:S(2)}) copy-start(f32[256,256]{1,0:T(8,128)S(1)} %fusion.20) | copy-start | bytes 786436
  106.2 9.8 %copy-start.6 = (f32[512,256]{1,0:T(8,128)}, f32[512,256]{1,0:T(8,128)S(1)}, u32[]{:S(2)}) copy-start(f32[512,256]{1,0:T(8,128)S(1)} %collective-permute-done.8) | copy-start | bytes 1572868
  107.7 45.9 %reduce-scatter.18.cloned.1.call-start = ((), (), s32[]{:S(2)}) async-start(), calls=%async_computation.14 | async-start | bytes 786432 | tf_op jit(solution)/shard_map/reduce_scatter | solution.py:79
  108.9 37.3 %copy-start.1 = (f32[256,512]{1,0:T(8,128)}, f32[256,512]{1,0:T(8,128)S(1)}, u32[]{:S(2)}) copy-start(f32[256,512]{1,0:T(8,128)S(1)} %broadcast_select_fusion.9) | copy-start | bytes 1572868
  108.9 30.1 %collective-permute-start.10 = (f32[256,512]{1,0:T(8,128)S(1)}, f32[256,512]{1,0:T(8,128)}, u32[]{:S(2)}, u32[]{:S(2)}) collective-permute-start(f32[256,512]{1,0:T(8,128)S(1)} %broadcast_select_fusion.9), channel_id=1, source_target_pairs={{0,8},{2,10},{4,12},{6,14},{8,0},{10,2},{12,4},{14,6},{16,24},{18,... | collective-permute-start | bytes 1572872 | tf_op jit(solution)/shard_map/ppermute | solution.py:10
  110.7 18.8 %collective-permute-start.7 = (f32[256,256]{1,0:T(8,128)}, f32[256,256]{1,0:T(8,128)}, u32[]{:S(2)}, u32[]{:S(2)}) collective-permute-start(f32[256,256]{1,0:T(8,128)} %get-tuple-element.4), channel_id=1, source_target_pairs={{0,8},{2,10},{4,12},{6,14},{8,0},{10,2},{12,4},{14,6},{16,24},{18,... | collective-permute-start | bytes 786440 | tf_op jit(solution)/shard_map/ppermute | solution.py:10
  116.0 18.9 %collective-permute-start.9 = (f32[256,256]{1,0:T(8,128)}, f32[256,256]{1,0:T(8,128)S(1)}, u32[]{:S(2)}, u32[]{:S(2)}) collective-permute-start(f32[256,256]{1,0:T(8,128)} %reduce-scatter.16.cloned.1.call-done), channel_id=1, source_target_pairs={{0,8},{2,10},{4,12},{6,14},{8,0},{10,2},{12,4},{14,6},{16,24},{18,... | collective-permute-start | bytes 786440 | tf_op jit(solution)/shard_map/ppermute | solution.py:10
  118.8 25.0 %collective-permute-start.12 = (f32[512,256]{1,0:T(8,128)S(1)}, f32[512,256]{1,0:T(8,128)S(1)}, u32[]{:S(2)}, u32[]{:S(2)}) collective-permute-start(f32[512,256]{1,0:T(8,128)S(1)} %broadcast_select_fusion.7), channel_id=1, source_target_pairs={{0,8},{2,10},{4,12},{6,14},{8,0},{10,2},{12,4},{14,6},{16,24},{18,... | collective-permute-start | bytes 1572872 | tf_op jit(solution)/shard_map/ppermute | solution.py:10
  139.7 4.2 %copy-start.13 = (f32[256,256]{1,0:T(8,128)}, f32[256,256]{1,0:T(8,128)S(1)}, u32[]{:S(2)}) copy-start(f32[256,256]{1,0:T(8,128)S(1)} %fusion.23) | copy-start | bytes 786436
  146.2 79.7 %reduce-scatter.20.cloned.1.call-start = ((), (), s32[]{:S(2)}) async-start(), calls=%async_computation.15 | async-start | bytes 786432 | tf_op jit(solution)/shard_map/reduce_scatter | solution.py:79
  147.4 62.1 %collective-permute-start.14 = (f32[256,512]{1,0:T(8,128)S(1)}, f32[256,512]{1,0:T(8,128)}, u32[]{:S(2)}, u32[]{:S(2)}) collective-permute-start(f32[256,512]{1,0:T(8,128)S(1)} %broadcast_select_fusion.5), channel_id=1, source_target_pairs={{0,16},{2,18},{4,20},{6,22},{8,24},{10,26},{12,28},{14,30},{16,0},... | collective-permute-start | bytes 1572872 | tf_op jit(solution)/shard_map/ppermute | solution.py:10
  150.1 50.5 %collective-permute-start.11 = (f32[256,256]{1,0:T(8,128)}, f32[256,256]{1,0:T(8,128)}, u32[]{:S(2)}, u32[]{:S(2)}) collective-permute-start(f32[256,256]{1,0:T(8,128)} %get-tuple-element.2), channel_id=1, source_target_pairs={{0,16},{2,18},{4,20},{6,22},{8,24},{10,26},{12,28},{14,30},{16,0},... | collective-permute-start | bytes 786440 | tf_op jit(solution)/shard_map/ppermute | solution.py:10
  153.6 52.5 %collective-permute-start.13 = (f32[256,256]{1,0:T(8,128)}, f32[256,256]{1,0:T(8,128)S(1)}, u32[]{:S(2)}, u32[]{:S(2)}) collective-permute-start(f32[256,256]{1,0:T(8,128)} %reduce-scatter.18.cloned.1.call-done), channel_id=1, source_target_pairs={{0,16},{2,18},{4,20},{6,22},{8,24},{10,26},{12,28},{14,30},{16,0},... | collective-permute-start | bytes 786440 | tf_op jit(solution)/shard_map/ppermute | solution.py:10
  157.3 58.8 %copy-start.8 = (f32[512,256]{1,0:T(8,128)}, f32[512,256]{1,0:T(8,128)S(1)}, u32[]{:S(2)}) copy-start(f32[512,256]{1,0:T(8,128)S(1)} %broadcast_select_fusion.3) | copy-start | bytes 1572868
  157.3 58.8 %collective-permute-start.15 = (f32[512,256]{1,0:T(8,128)S(1)}, f32[512,256]{1,0:T(8,128)S(1)}, u32[]{:S(2)}, u32[]{:S(2)}) collective-permute-start(f32[512,256]{1,0:T(8,128)S(1)} %broadcast_select_fusion.3), channel_id=1, source_target_pairs={{0,16},{2,18},{4,20},{6,22},{8,24},{10,26},{12,28},{14,30},{16,0},... | collective-permute-start | bytes 1572872 | tf_op jit(solution)/shard_map/ppermute | solution.py:10
  210.1 6.1 %copy-start.14 = (f32[256,256]{1,0:T(8,128)}, f32[256,256]{1,0:T(8,128)S(1)}, u32[]{:S(2)}) copy-start(f32[256,256]{1,0:T(8,128)S(1)} %fusion.26) | copy-start | bytes 786436
  218.4 22.2 %reduce-scatter.22.cloned.1.call-start = ((), (), s32[]{:S(2)}) async-start(), calls=%async_computation.16 | async-start | bytes 786432 | tf_op jit(solution)/shard_map/reduce_scatter | solution.py:97
  233.3 23.4 %reduce-scatter.24.cloned.1.call-start = ((), (), s32[]{:S(2)}) async-start(), calls=%async_computation.17 | async-start | bytes 786432 | tf_op jit(solution)/shard_map/reduce_scatter | solution.py:97
  246.4 26.2 %reduce-scatter.26.cloned.1.call-start = ((), (), s32[]{:S(2)}) async-start(), calls=%async_computation.18 | async-start | bytes 786432 | tf_op jit(solution)/shard_map/reduce_scatter | solution.py:97
  260.6 30.2 %copy-start.3 = (f32[1,512,256]{2,1,0:T(8,128)S(1)}, f32[1,512,256]{2,1,0:T(8,128)}, u32[]{:S(2)}) copy-start(f32[1,512,256]{2,1,0:T(8,128)} %param.11) | copy-start | bytes 1572868
  260.6 30.2 %copy-start.5 = (f32[512,256]{1,0:T(8,128)S(1)}, f32[512,256]{1,0:T(8,128)}, u32[]{:S(2)}) copy-start(f32[512,256]{1,0:T(8,128)} %copy-done.4) | copy-start | bytes 1572868
  263.2 25.2 %reduce-scatter.28.cloned.1.call-start = ((), (), s32[]{:S(2)}) async-start(), calls=%async_computation.19 | async-start | bytes 786432 | tf_op jit(solution)/shard_map/reduce_scatter | solution.py:97
  276.5 15.0 %copy-start.10 = (f32[1,256,512]{2,1,0:T(8,128)S(1)}, f32[1,256,512]{2,1,0:T(8,128)}, u32[]{:S(2)}) copy-start(f32[1,256,512]{2,1,0:T(8,128)} %param.10) | copy-start | bytes 1572868
  278.0 25.2 %reduce-scatter.30.cloned.1.call-start = ((), (), s32[]{:S(2)}) async-start(), calls=%async_computation.20 | async-start | bytes 786432 | tf_op jit(solution)/shard_map/reduce_scatter | solution.py:97
  293.0 28.9 %reduce-scatter.32.cloned.1.call-start = ((), (), s32[]{:S(2)}) async-start(), calls=%async_computation.21 | async-start | bytes 3145728 | tf_op jit(solution)/shard_map/reduce_scatter | solution.py:105
  305.6 5.4 %copy-start.16 = (f32[256,256]{1,0:T(8,128)S(1)}, f32[256,256]{1,0:T(8,128)}, u32[]{:S(2)}) copy-start(f32[256,256]{1,0:T(8,128)} %reduce-scatter.22.cloned.1.call-done) | copy-start | bytes 786436
  305.6 5.4 %copy-start.17 = (f32[256,256]{1,0:T(8,128)S(1)}, f32[256,256]{1,0:T(8,128)}, u32[]{:S(2)}) copy-start(f32[256,256]{1,0:T(8,128)} %reduce-scatter.24.cloned.1.call-done) | copy-start | bytes 786436
  305.6 5.4 %copy-start.18 = (f32[256,256]{1,0:T(8,128)S(1)}, f32[256,256]{1,0:T(8,128)}, u32[]{:S(2)}) copy-start(f32[256,256]{1,0:T(8,128)} %reduce-scatter.26.cloned.1.call-done) | copy-start | bytes 786436
  305.6 5.4 %copy-start.19 = (f32[256,256]{1,0:T(8,128)S(1)}, f32[256,256]{1,0:T(8,128)}, u32[]{:S(2)}) copy-start(f32[256,256]{1,0:T(8,128)} %reduce-scatter.28.cloned.1.call-done) | copy-start | bytes 786436
  305.6 5.4 %copy-start.20 = (f32[256,256]{1,0:T(8,128)S(1)}, f32[256,256]{1,0:T(8,128)}, u32[]{:S(2)}) copy-start(f32[256,256]{1,0:T(8,128)} %reduce-scatter.30.cloned.1.call-done) | copy-start | bytes 786436
  (3 other events, 2.4 us)
Sparse Core Ops, SparseCore 0:
  9.5 11.7 all-gather.2
  27.4 9.0 reduce-scatter.11
  69.3 9.0 reduce-scatter.13
  107.8 8.1 reduce-scatter.15
  146.3 7.2 reduce-scatter.17
  218.6 7.2 reduce-scatter.19
  233.4 7.1 reduce-scatter.21
  246.5 10.0 reduce-scatter.23
  263.3 9.1 reduce-scatter.25
  278.1 10.2 reduce-scatter.27
  293.1 10.0 reduce-scatter.29
  311.1 10.7 reduce-scatter.31
where the time goes:
time: 329 us
  waiting for transfers between devices  219 us (67%)
  matrix products  35.3 us (11%)
  blocking collectives  22.9 us (7%)
  starting transfers between devices  20.3 us (6%)
  between operations  14.6 us (4%)
  other arithmetic  14.3 us (4%)
    ppermute x16, waiting for transfers between devices, partner(): return lax.ppermute(value, axis, pairs)  118 us
    reduce_scatter x5, waiting for transfers between devices, local(): lax.psum_scatter(partial_value, 'sep', scatter_dimension=1, tiled=True)  47.4 us
    reduce_scatter x5, waiting for transfers between devices, local(): share = lax.psum_scatter(mine, 'sep', scatter_dimension=1, tiled=True)  29 us
    ppermute x16, starting transfers between devices, partner(): return lax.ppermute(value, axis, pairs)  19.9 us
    dot_general x9, matrix products, times_plain(): jnp.dot(left, right, precision=lax.Precision.HIGHEST, preferred_element_t...  14.9 us
    all_gather x1, waiting for transfers between devices, local(): lax.all_gather(rhs_local, 'sep', axis=1, tiled=True)  13.3 us
    all_gather x5, blocking collectives, local(): parent_full = lax.all_gather(current, 'sep', axis=1, tiled=True)  12.1 us
    all_gather x5, blocking collectives, local(): whole_work = lax.all_gather(rhs_half - total, 'sep', axis=1, tiled=True)  10.9 us
  transfers between devices with their start and end apart: 28, of which 24 were waited for; matrix products, arithmetic and copies ran while one was open for 5% of the time, Pallas kernels for 0%

commit v1 on v0

v1 whole, which is shorter than its diff:
```python
import jax
import jax.numpy as jnp
from jax import lax
from jax.sharding import PartitionSpec as P

ROWS = (((1,), (0,)), ((), ()))
BOTH = (((1,), (1,)), ((), ()))
FIRST = (((0,), (0,)), ((), ()))


def product(left, right, dims, precision=lax.Precision.HIGH):
    return lax.dot_general(
        left, right, dims, precision=precision, preferred_element_type=jnp.float32
    )


def swap(value):
    pairs = [(source, source ^ 1) for source in range(lax.axis_size("sep"))]
    return lax.ppermute(value, "sep", pairs)


def send(value, pairs):
    return lax.ppermute(value.astype(jnp.bfloat16), "leaf", pairs).astype(jnp.float32)


def join(mine, other, first, axis):
    return jnp.where(
        first,
        jnp.concatenate([mine, other], axis=axis),
        jnp.concatenate([other, mine], axis=axis),
    )


def local(leaf_rhs, leaf_inv, leaf_couple, sep_rhs, sep_inv, sep_couple):
    count = lax.axis_size("leaf")
    depth = count.bit_length() - 1
    place = lax.axis_index("leaf")
    core = lax.axis_index("sep")
    first = core == 0
    even = place % 2 == 0
    inv_rows = leaf_inv[0]
    couple_cols = leaf_couple[0]
    half = leaf_rhs.shape[1] // 2
    half_sep = sep_rhs.shape[2]
    top, below = count - 1, count // 2 - 1

    def my_rows(value):
        return lax.dynamic_slice_in_dim(value, core * half, half, 0)

    def other_rows(value):
        return lax.dynamic_slice_in_dim(value, (1 - core) * half, half, 0)

    rhs_full = join(leaf_rhs[0], swap(leaf_rhs[0]), first, 1)
    leaf_state = lax.dot_general(
        rhs_full, inv_rows, BOTH, preferred_element_type=jnp.float32
    ).astype(jnp.bfloat16)
    theirs = product(other_rows(leaf_state), couple_cols, BOTH, None)
    ours = product(my_rows(leaf_state), couple_cols, BOTH, None)

    sep_local = sep_rhs[0]
    rhs_rows = join(my_rows(sep_local), swap(other_rows(sep_local)), first, 1)
    inv_half = sep_inv[0]
    inverse = join(inv_half, swap(inv_half), first, 0)
    couple = join(sep_couple[0], swap(sep_couple[0]), first, 1)
    pull = product(couple, inverse, ROWS, lax.Precision.HIGHEST)
    gram = product(inverse, inverse, FIRST, lax.Precision.HIGHEST)
    top_rhs = lax.ppermute(rhs_rows, "leaf", [(top, below)])
    top_half = lax.ppermute(inv_half, "leaf", [(top, below)])
    top_inverse = join(top_half, swap(top_half), first, 0)
    top_gram = product(top_inverse, top_inverse, FIRST, lax.Precision.HIGHEST)

    outgoing = ours + swap(theirs)
    work = rhs_rows - jnp.where(even, outgoing, 0.0)
    work = work - send(outgoing, [(k + 1, k) for k in range(0, count, 2)])
    for level in range(1, depth):
        reach = 2 ** (level - 1)
        parents = range(2 * reach - 1, count, 4 * reach)
        outgoing = product(work, pull, BOTH)
        lower = send(outgoing, [(k - reach, k) for k in parents])
        upper = send(outgoing, [(k + reach, k) for k in parents])
        work = work - (lower + upper)
    top_work = top_rhs - product(work, pull, BOTH)
    top_solution = product(top_work, top_gram, ROWS)
    parent = top_solution
    state = product(work, gram, ROWS)
    for level in range(depth, 1, -1):
        reach = 2 ** (level - 2)
        slots = range(2 * reach - 1, count, 4 * reach)
        solved = state - product(parent, pull, ROWS)
        lower = send(solved, [(k, k - reach) for k in slots])
        upper = send(solved, [(k, k + reach) for k in slots])
        parent = parent + (lower + upper)
    solved = state - product(parent, pull, ROWS)
    beside = lax.ppermute(
        solved.astype(jnp.bfloat16), "leaf", [(k, k + 1) for k in range(0, count, 2)]
    )
    parent_rows = jnp.where(even, solved.astype(jnp.bfloat16), beside)

    parent_full = join(parent_rows, swap(parent_rows), first, 0)
    pulled = jnp.dot(parent_full, couple_cols, preferred_element_type=jnp.float32)
    residue = (leaf_state.astype(jnp.float32) - pulled).astype(jnp.bfloat16)
    spread = jnp.dot(residue, inv_rows, preferred_element_type=jnp.float32)
    wide = leaf_rhs.shape[2]
    away = lax.dynamic_slice_in_dim(spread, (1 - core) * wide, wide, 1)
    here = lax.dynamic_slice_in_dim(spread, core * wide, wide, 1)
    leaf_solution = here + swap(away)

    from_below = lax.ppermute(top_solution, "leaf", [(below, top)])
    whole = jnp.where(place == top, from_below, solved)
    away = lax.dynamic_slice_in_dim(whole, (1 - core) * half_sep, half_sep, 1)
    here = lax.dynamic_slice_in_dim(whole, core * half_sep, half_sep, 1)
    sep_solution = join(here, swap(away), first, 0)
    return (leaf_solution[None], sep_solution[None])


def solution(mesh):
    return jax.shard_map(
        local,
        mesh=mesh,
        in_specs=(
            P("leaf", None, "sep"),
            P("leaf", "sep", None),
            P("leaf", None, "sep"),
            P("leaf", None, "sep"),
            P("leaf", "sep", None),
            P("leaf", None, "sep"),
        ),
        out_specs=(P("leaf", None, "sep"), P("leaf", None, "sep")),
        check_vma=False,
    )
```

time: 329 us -> 91 us (0.28)
  waiting for transfers between devices: 219 us -> 39.9 us
  blocking collectives: 22.9 us -> 0 us
  between operations: 14.6 us -> 1.11 us
  other arithmetic: 14.3 us -> 3.25 us
  matrix products: 35.3 us -> 26 us
    reduce_scatter x11 -> x0, waiting for transfers between devices: 86.4 us -> none  [the longest x5 47.4 us: local(): lax.psum_scatter(partial_value, 'sep', scatter_dimension=1, tiled=True)]
    ppermute x16 -> x26, waiting for transfers between devices: 118 us -> 39.9 us  [the longest x13 32.2 us: send(): lax.ppermute(value.astype(jnp.bfloat16), 'leaf', pairs).astype(jnp.float32)]
    all_gather x10 -> x0, blocking collectives: 22.9 us -> none  [the longest x5 12.1 us: local(): parent_full = lax.all_gather(current, 'sep', axis=1, tiled=True)]
    all_gather x1 -> x0, waiting for transfers between devices: 13.3 us -> none  [local(): lax.all_gather(rhs_local, 'sep', axis=1, tiled=True)]
    select_n x9 -> x3, other arithmetic: 11.3 us -> 0.78 us  [the longest x1 0.73 us: join(): jnp.where(first, jnp.concatenate([mine, other], axis=axis), jnp.concatena...]
    dot_general x20 -> x16, matrix products: 29.9 us -> 21.9 us  [the longest x15 18.1 us: product(): lax.dot_general(left, right, dims, precision=precision, preferred_element...]
    ppermute x16 -> x26, starting transfers between devices: 19.9 us -> 18.6 us  [the longest x13 12 us: send(): lax.ppermute(value.astype(jnp.bfloat16), 'leaf', pairs).astype(jnp.float32)]
  transfers between devices with their start and end apart: 28 -> 26, of which waited for: 24 -> 7; matrix products, arithmetic and copies ran while one was open for 5% -> 19% of each run, Pallas kernels for 0% -> 0%
where the time goes in v1:
time: 91 us; the launch traced here: 90.6 us
  waiting for transfers between devices  39.9 us (44%)
  matrix products  26 us (29%)
  starting transfers between devices  18.6 us (20%)
  other arithmetic  3.25 us (4%)
  local copies, waits for them, and re-layouts  1.76 us (2%)
  between operations  1.11 us (1%)
    ppermute x13, waiting for transfers between devices, send(): lax.ppermute(value.astype(jnp.bfloat16), 'leaf', pairs).astype(jnp.float32)  32.2 us
    dot_general x15, matrix products, product(): lax.dot_general(left, right, dims, precision=precision, preferred_element...  18.1 us
    ppermute x13, starting transfers between devices, send(): lax.ppermute(value.astype(jnp.bfloat16), 'leaf', pairs).astype(jnp.float32)  12 us
    ppermute x9, waiting for transfers between devices, swap(): return lax.ppermute(value, 'sep', pairs)  5.1 us
    dot_general x1, matrix products, local(): spread = jnp.dot(residue, inv_rows, preferred_element_type=jnp.float32)  4.02 us
    dot_general x1, matrix products, local(): lax.dot_general(rhs_full, inv_rows, BOTH, preferred_element_type=jnp.floa...  3.8 us
    ppermute x1, waiting for transfers between devices, local(): lax.ppermute(solved.astype(jnp.bfloat16), 'leaf', [(k, k + 1) for k in ra...  2.5 us
    ppermute x9, starting transfers between devices, swap(): return lax.ppermute(value, 'sep', pairs)  2.36 us
  transfers between devices with their start and end apart: 26, of which 7 were waited for; matrix products, arithmetic and copies ran while one was open for 19% of the time, Pallas kernels for 0%

profile of v1, /device:TPU:0, one launch (start us, length us, event | category | flops | bytes accessed | tf_op | source)
XLA Modules:
  0.0 90.6 jit_solution(6960039177324128255)
XLA Ops:
  0.6 0.6 collective-permute-start
  1.2 1.7 %collective-permute-done = bf16[256,1024]{1,0:T(8,128)(2,1)S(1)} collective-permute-done((bf16[256,1024]{1,0:T(8,128)(2,1)}, bf16[256,1024]{1,0:T(8,128)(2,1)S(1)}, u32[]{:S(2)}, u32[]{:S(2)}) %collective-permute-start) | collective-permute-done | bytes 524320 | tf_op jit(solution)/shard_map/ppermute | solution.py:19
  3.0 3.8 %fusion.5 = bf16[256,1024]{1,0:T(8,128)(2,1)S(1)} fusion(bf16[1,1024,2048]{2,1,0:T(8,128)(2,1)} %param.7, bf16[256,1024]{1,0:T(8,128)(2,1)S(1)} %collective-permute-done, bf16[256,1024]{1,0:T(8,128)(2,1)} %bitcast.45, pred[]{:T(512)S(6)} %eq.11), kind=kOutput, calls=%fused_computation.6 | convolution fusion | flops 1078722560 | bytes 5767169 | tf_op jit(solution)/shard_map/dot_general | solution.py:54
  6.8 0.5 fusion.29
  7.3 0.4 collective-permute-start.2
  7.9 0.4 collective-permute-start.4
  8.2 1.5 %collective-permute-start.13 = (f32[256,512]{1,0:T(8,128)}, f32[256,512]{1,0:T(8,128)}, u32[]{:S(2)}, u32[]{:S(2)}) collective-permute-start(f32[256,512]{1,0:T(8,128)} %bitcast.6), channel_id=1, source_target_pairs={{30,14},{31,15}} | collective-permute-start | bytes 1572872 | tf_op jit(solution)/shard_map/ppermute | solution.py:68
  9.9 0.5 fusion.69
  10.4 1.3 %collective-permute-start.3 = (bf16[128,512]{1,0:T(8,128)(2,1)S(1)}, bf16[128,512]{1,0:T(8,128)(2,1)S(1)}, u32[]{:S(2)}, u32[]{:S(2)}) collective-permute-start(bf16[128,512]{1,0:T(8,128)(2,1)S(1)} %get-tuple-element.10), channel_id=1, source_target_pairs={{2,0},{6,4},{10,8},{14,12},{18,16},{22,20},{26,24},{30,28},{3,1},{... | collective-permute-start | bytes 393224 | tf_op jit(solution)/shard_map/ppermute | solution.py:23
  11.7 3.7 %fusion.16 = f32[512,512]{1,0:T(8,128)S(1)} fusion(f32[512,256]{1,0:T(8,128)} %collective-permute-done.4, f32[512,256]{1,0:T(8,128)S(1)} %bitcast.47, f32[256,512]{1,0:T(8,128)} %collective-permute-done.5, f32[256,512]{1,0:T(8,128)} %bitcast.6, pred[]{:T(512)S(6)} %eq.11), kind=kOutput, calls=%fused_computation.25 | convolution fusion | flops 1612185600 | bytes 3145729 | tf_op jit(solution)/shard_map/dot_general | solution.py:12
  15.5 2.9 %collective-permute-done.3 = bf16[128,512]{1,0:T(8,128)(2,1)S(1)} collective-permute-done((bf16[128,512]{1,0:T(8,128)(2,1)S(1)}, bf16[128,512]{1,0:T(8,128)(2,1)S(1)}, u32[]{:S(2)}, u32[]{:S(2)}) %collective-permute-start.3) | collective-permute-done | bytes 131104 | tf_op jit(solution)/shard_map/ppermute | solution.py:23
  18.4 0.7 convolution_convert_fusion.2
  19.1 0.7 collective-permute-start.7
  19.7 2.6 %collective-permute-start.6 = (bf16[128,512]{1,0:T(8,128)(2,1)S(1)}, bf16[128,512]{1,0:T(8,128)(2,1)S(1)}, u32[]{:S(2)}, u32[]{:S(2)}) collective-permute-start(bf16[128,512]{1,0:T(8,128)(2,1)S(1)} %convolution_convert_fusion.2), channel_id=1, source_target_pairs={{0,2},{8,10},{16,18},{24,26},{1,3},{9,11},{17,19},{25,27}} | collective-permute-start | bytes 393224 | tf_op jit(solution)/shard_map/ppermute | solution.py:23
  22.4 2.9 %collective-permute-done.6 = bf16[128,512]{1,0:T(8,128)(2,1)S(1)} collective-permute-done((bf16[128,512]{1,0:T(8,128)(2,1)S(1)}, bf16[128,512]{1,0:T(8,128)(2,1)S(1)}, u32[]{:S(2)}, u32[]{:S(2)}) %collective-permute-start.6) | collective-permute-done | bytes 131104 | tf_op jit(solution)/shard_map/ppermute | solution.py:23
  25.3 0.7 convolution_convert_fusion.1
  26.0 0.7 collective-permute-start.9
  26.7 0.7 collective-permute-start.8
  27.4 4.4 %fusion.35 = f32[512,512]{1,0:T(8,128)S(1)} fusion(f32[256,512]{1,0:T(8,128)} %collective-permute-done.5, f32[256,512]{1,0:T(8,128)} %bitcast.6, pred[]{:T(512)S(6)} %eq.11), kind=kOutput, calls=%fused_computation.45 | convolution fusion | flops 1611399168 | bytes 2097153 | tf_op jit(solution)/shard_map/dot_general | solution.py:12
  31.8 0.7 collective-permute-start.12
  32.6 0.7 convolution_convert_fusion
  33.2 0.7 collective-permute-start.11
  33.9 0.8 collective-permute-start.10
  34.8 3.6 %fusion.22 = f32[512,512]{1,0:T(8,128)S(1)} fusion(f32[256,512]{1,0:T(8,128)S(1)} %collective-permute-done.14, f32[256,512]{1,0:T(8,128)} %collective-permute-done.13, pred[]{:T(512)S(6)} %eq.11), kind=kOutput, calls=%fused_computation.33 | convolution fusion | flops 1611399168 | bytes 2097153 | tf_op jit(solution)/shard_map/dot_general | solution.py:12
  38.4 0.7 fusion.59
  39.1 0.5 fusion.60
  39.6 0.5 fusion.53
  40.1 0.4 fusion.8
  40.5 0.7 collective-permute-start.16
  41.2 0.7 collective-permute-start.15
  41.9 0.4 fusion.9
  42.3 0.7 collective-permute-start.18
  43.0 0.7 collective-permute-start.17
  43.7 0.5 fusion.10
  44.2 0.7 collective-permute-start.20
  44.8 1.3 %collective-permute-start.19 = (bf16[128,512]{1,0:T(8,128)(2,1)S(1)}, bf16[128,512]{1,0:T(8,128)(2,1)S(1)}, u32[]{:S(2)}, u32[]{:S(2)}) collective-permute-start(bf16[128,512]{1,0:T(8,128)(2,1)S(1)} %fusion.10), channel_id=1, source_target_pairs={{2,0},{10,8},{18,16},{26,24},{3,1},{11,9},{19,17},{27,25}} | collective-permute-start | bytes 393224 | tf_op jit(solution)/shard_map/ppermute | solution.py:23
  46.2 0.7 collective-permute-start.24
  46.8 26.4 %collective-permute-done.19 = bf16[128,512]{1,0:T(8,128)(2,1)S(1)} collective-permute-done((bf16[128,512]{1,0:T(8,128)(2,1)S(1)}, bf16[128,512]{1,0:T(8,128)(2,1)S(1)}, u32[]{:S(2)}, u32[]{:S(2)}) %collective-permute-start.19) | collective-permute-done | bytes 131104 | tf_op jit(solution)/shard_map/ppermute | solution.py:23
  73.3 0.5 convolution_subtract_fusion.1
  73.8 1.5 %collective-permute-start.21 = (bf16[128,512]{1,0:T(8,128)(2,1)S(1)}, bf16[128,512]{1,0:T(8,128)(2,1)S(1)}, u32[]{:S(2)}, u32[]{:S(2)}) collective-permute-start(bf16[128,512]{1,0:T(8,128)(2,1)S(1)} %get-tuple-element.7), channel_id=1, source_target_pairs={{0,2},{4,6},{8,10},{12,14},{16,18},{20,22},{24,26},{28,30},{1,3},{... | collective-permute-start | bytes 393224 | tf_op jit(solution)/shard_map/ppermute | solution.py:94
  75.3 2.5 %collective-permute-done.21 = bf16[128,512]{1,0:T(8,128)(2,1)S(1)} collective-permute-done((bf16[128,512]{1,0:T(8,128)(2,1)S(1)}, bf16[128,512]{1,0:T(8,128)(2,1)S(1)}, u32[]{:S(2)}, u32[]{:S(2)}) %collective-permute-start.21) | collective-permute-done | bytes 131104 | tf_op jit(solution)/shard_map/ppermute | solution.py:94
  77.9 1.5 %collective-permute-done.22 = bf16[128,512]{1,0:T(8,128)(2,1)} collective-permute-done((bf16[128,512]{1,0:T(8,128)(2,1)S(1)}, bf16[128,512]{1,0:T(8,128)(2,1)}, u32[]{:S(2)}, u32[]{:S(2)}) %collective-permute-start.22) | collective-permute-done | bytes 131104 | tf_op jit(solution)/shard_map/ppermute | solution.py:19
  79.4 4.0 %fusion = f32[256,2048]{1,0:T(8,128)S(1)} fusion(bf16[1,1024,2048]{2,1,0:T(8,128)(2,1)} %param.7, bf16[1,512,1024]{2,1,0:T(8,128)(2,1)S(1)} %copy-done, bf16[256,1024]{1,0:T(8,128)(2,1)} %copy-done.1, bf16[128,512]{1,0:T(8,128)(2,1)} %collective-permute-done.22, bf16[128,512]{1,0:T(8,128)(2,1)S(1)} %broadcast_select_fusion.1, pred[]{:T(512)S(6)} %eq.11), kind=kOutput, calls=%fused_computation | convolution fusion | flops 1344143360 | bytes 8126465 | tf_op jit(solution)/shard_map/dot_general | solution.py:102
  83.4 1.1 %constant_dynamic-slice_fusion.1 = f32[256,1024]{1,0:T(8,128)} fusion(f32[256,2048]{1,0:T(8,128)S(1)} %fusion, s32[]{:T(128)S(6)} %select_n.119), kind=kLoop, calls=%fused_computation.80 | loop fusion | bytes 2097156 | tf_op jit(solution)/shard_map/dynamic_slice | solution.py:104
  84.6 0.7 dynamic-slice_bitcast_fusion
  85.6 1.9 %collective-permute-done.25 = f32[128,256]{1,0:T(8,128)S(1)} collective-permute-done((f32[128,256]{1,0:T(8,128)}, f32[128,256]{1,0:T(8,128)S(1)}, u32[]{:S(2)}, u32[]{:S(2)}) %collective-permute-start.25) | collective-permute-done | bytes 131104 | tf_op jit(solution)/shard_map/ppermute | solution.py:19
  87.5 0.7 maximum_select_fusion.13
  88.2 2.3 %add_bitcast_fusion = f32[1,256,1024]{2,1,0:T(8,128)} fusion(f32[256,1024]{1,0:T(8,128)} %collective-permute-done.23, f32[256,2048]{1,0:T(8,128)S(1)} %fusion, s32[]{:T(128)S(6)} %select_n.118), kind=kLoop, calls=%fused_computation.43 | loop fusion | flops 262144 | bytes 3145732 | tf_op jit(solution)/shard_map/broadcast_in_dim | solution.py:113
  (38 shorter events, 1.3 us)
Async XLA Ops:
  0.6 6.1 %copy-start = (bf16[1,512,1024]{2,1,0:T(8,128)(2,1)S(1)}, bf16[1,512,1024]{2,1,0:T(8,128)(2,1)}, u32[]{:S(2)}) copy-start(bf16[1,512,1024]{2,1,0:T(8,128)(2,1)} %param.8) | copy-start | bytes 3145732
  0.6 2.3 %collective-permute-start = (bf16[256,1024]{1,0:T(8,128)(2,1)}, bf16[256,1024]{1,0:T(8,128)(2,1)S(1)}, u32[]{:S(2)}, u32[]{:S(2)}) collective-permute-start(bf16[256,1024]{1,0:T(8,128)(2,1)} %bitcast.44), channel_id=1, source_target_pairs={{0,1},{1,0},{2,3},{3,2},{4,5},{5,4},{6,7},{7,6},{8,9},{9,8},{10,11... | collective-permute-start | bytes 1572872 | tf_op jit(solution)/shard_map/ppermute | solution.py:19
  1.2 6.6 %copy-start.3 = (f32[1,512,256]{2,1,0:T(8,128)S(1)}, f32[1,512,256]{2,1,0:T(8,128)}, u32[]{:S(2)}) copy-start(f32[1,512,256]{2,1,0:T(8,128)} %param.11) | copy-start | bytes 1572868
  1.2 8.5 %copy-start.2 = (f32[1,256,256]{2,1,0:T(8,128)S(1)}, f32[1,256,256]{2,1,0:T(8,128)}, u32[]{:S(2)}) copy-start(f32[1,256,256]{2,1,0:T(8,128)} %param.9) | copy-start | bytes 786436
  6.8 5.0 %copy-start.1 = (bf16[256,1024]{1,0:T(8,128)(2,1)}, bf16[256,1024]{1,0:T(8,128)(2,1)S(1)}, u32[]{:S(2)}) copy-start(bf16[256,1024]{1,0:T(8,128)(2,1)S(1)} %fusion.5) | copy-start | bytes 1572868
  7.3 2.6 %collective-permute-start.2 = (f32[128,512]{1,0:T(8,128)S(1)}, f32[128,512]{1,0:T(8,128)S(1)}, u32[]{:S(2)}, u32[]{:S(2)}) collective-permute-start(f32[128,512]{1,0:T(8,128)S(1)} %fusion.29), channel_id=1, source_target_pairs={{0,1},{1,0},{2,3},{3,2},{4,5},{5,4},{6,7},{7,6},{8,9},{9,8},{10,11... | collective-permute-start | bytes 786440 | tf_op jit(solution)/shard_map/ppermute | solution.py:19
  7.7 4.0 %collective-permute-start.5 = (f32[256,512]{1,0:T(8,128)}, f32[256,512]{1,0:T(8,128)}, u32[]{:S(2)}, u32[]{:S(2)}) collective-permute-start(f32[256,512]{1,0:T(8,128)} %bitcast.6), channel_id=1, source_target_pairs={{0,1},{1,0},{2,3},{3,2},{4,5},{5,4},{6,7},{7,6},{8,9},{9,8},{10,11... | collective-permute-start | bytes 1572872 | tf_op jit(solution)/shard_map/ppermute | solution.py:19
  7.9 3.9 %collective-permute-start.4 = (f32[512,256]{1,0:T(8,128)S(1)}, f32[512,256]{1,0:T(8,128)}, u32[]{:S(2)}, u32[]{:S(2)}) collective-permute-start(f32[512,256]{1,0:T(8,128)S(1)} %bitcast.46), channel_id=1, source_target_pairs={{0,1},{1,0},{2,3},{3,2},{4,5},{5,4},{6,7},{7,6},{8,9},{9,8},{10,11... | collective-permute-start | bytes 1572872 | tf_op jit(solution)/shard_map/ppermute | solution.py:19
  8.2 14.1 %collective-permute-start.13 = (f32[256,512]{1,0:T(8,128)}, f32[256,512]{1,0:T(8,128)}, u32[]{:S(2)}, u32[]{:S(2)}) collective-permute-start(f32[256,512]{1,0:T(8,128)} %bitcast.6), channel_id=1, source_target_pairs={{30,14},{31,15}} | collective-permute-start | bytes 1572872 | tf_op jit(solution)/shard_map/ppermute | solution.py:68
  9.7 5.8 %collective-permute-start.1 = (f32[128,256]{1,0:T(8,128)S(1)}, f32[128,256]{1,0:T(8,128)S(1)}, u32[]{:S(2)}, u32[]{:S(2)}) collective-permute-start(f32[128,256]{1,0:T(8,128)S(1)} %get-tuple-element.8), channel_id=1, source_target_pairs={{0,1},{1,0},{2,3},{3,2},{4,5},{5,4},{6,7},{7,6},{8,9},{9,8},{10,11... | collective-permute-start | bytes 393224 | tf_op jit(solution)/shard_map/ppermute | solution.py:19
  10.4 7.9 %collective-permute-start.3 = (bf16[128,512]{1,0:T(8,128)(2,1)S(1)}, bf16[128,512]{1,0:T(8,128)(2,1)S(1)}, u32[]{:S(2)}, u32[]{:S(2)}) collective-permute-start(bf16[128,512]{1,0:T(8,128)(2,1)S(1)} %get-tuple-element.10), channel_id=1, source_target_pairs={{2,0},{6,4},{10,8},{14,12},{18,16},{22,20},{26,24},{30,28},{3,1},{... | collective-permute-start | bytes 393224 | tf_op jit(solution)/shard_map/ppermute | solution.py:23
  19.1 3.3 %collective-permute-start.7 = (bf16[128,512]{1,0:T(8,128)(2,1)S(1)}, bf16[128,512]{1,0:T(8,128)(2,1)S(1)}, u32[]{:S(2)}, u32[]{:S(2)}) collective-permute-start(bf16[128,512]{1,0:T(8,128)(2,1)S(1)} %convolution_convert_fusion.2), channel_id=1, source_target_pairs={{4,2},{12,10},{20,18},{28,26},{5,3},{13,11},{21,19},{29,27}} | collective-permute-start | bytes 393224 | tf_op jit(solution)/shard_map/ppermute | solution.py:23
  19.7 5.6 %collective-permute-start.6 = (bf16[128,512]{1,0:T(8,128)(2,1)S(1)}, bf16[128,512]{1,0:T(8,128)(2,1)S(1)}, u32[]{:S(2)}, u32[]{:S(2)}) collective-permute-start(bf16[128,512]{1,0:T(8,128)(2,1)S(1)} %convolution_convert_fusion.2), channel_id=1, source_target_pairs={{0,2},{8,10},{16,18},{24,26},{1,3},{9,11},{17,19},{25,27}} | collective-permute-start | bytes 393224 | tf_op jit(solution)/shard_map/ppermute | solution.py:23
  22.3 12.4 %collective-permute-start.14 = (f32[256,512]{1,0:T(8,128)}, f32[256,512]{1,0:T(8,128)S(1)}, u32[]{:S(2)}, u32[]{:S(2)}) collective-permute-start(f32[256,512]{1,0:T(8,128)} %collective-permute-done.13), channel_id=1, source_target_pairs={{0,1},{1,0},{2,3},{3,2},{4,5},{5,4},{6,7},{7,6},{8,9},{9,8},{10,11... | collective-permute-start | bytes 1572872 | tf_op jit(solution)/shard_map/ppermute | solution.py:19
  26.0 6.5 %collective-permute-start.9 = (bf16[128,512]{1,0:T(8,128)(2,1)S(1)}, bf16[128,512]{1,0:T(8,128)(2,1)S(1)}, u32[]{:S(2)}, u32[]{:S(2)}) collective-permute-start(bf16[128,512]{1,0:T(8,128)(2,1)S(1)} %convolution_convert_fusion.1), channel_id=1, source_target_pairs={{10,6},{26,22},{11,7},{27,23}} | collective-permute-start | bytes 393224 | tf_op jit(solution)/shard_map/ppermute | solution.py:23
  26.7 5.8 %collective-permute-start.8 = (bf16[128,512]{1,0:T(8,128)(2,1)S(1)}, bf16[128,512]{1,0:T(8,128)(2,1)S(1)}, u32[]{:S(2)}, u32[]{:S(2)}) collective-permute-start(bf16[128,512]{1,0:T(8,128)(2,1)S(1)} %convolution_convert_fusion.1), channel_id=1, source_target_pairs={{2,6},{18,22},{3,7},{19,23}} | collective-permute-start | bytes 393224 | tf_op jit(solution)/shard_map/ppermute | solution.py:23
  31.8 7.8 %collective-permute-start.12 = (f32[128,512]{1,0:T(8,128)S(1)}, f32[128,512]{1,0:T(8,128)S(1)}, u32[]{:S(2)}, u32[]{:S(2)}) collective-permute-start(f32[128,512]{1,0:T(8,128)S(1)} %get-tuple-element.3), channel_id=1, source_target_pairs={{30,14},{31,15}} | collective-permute-start | bytes 786440 | tf_op jit(solution)/shard_map/ppermute | solution.py:67
  33.2 5.2 %collective-permute-start.11 = (bf16[128,512]{1,0:T(8,128)(2,1)S(1)}, bf16[128,512]{1,0:T(8,128)(2,1)S(1)}, u32[]{:S(2)}, u32[]{:S(2)}) collective-permute-start(bf16[128,512]{1,0:T(8,128)(2,1)S(1)} %convolution_convert_fusion), channel_id=1, source_target_pairs={{22,14},{23,15}} | collective-permute-start | bytes 393224 | tf_op jit(solution)/shard_map/ppermute | solution.py:23
  33.9 4.5 %collective-permute-start.10 = (bf16[128,512]{1,0:T(8,128)(2,1)S(1)}, bf16[128,512]{1,0:T(8,128)(2,1)S(1)}, u32[]{:S(2)}, u32[]{:S(2)}) collective-permute-start(bf16[128,512]{1,0:T(8,128)(2,1)S(1)} %convolution_convert_fusion), channel_id=1, source_target_pairs={{6,14},{7,15}} | collective-permute-start | bytes 393224 | tf_op jit(solution)/shard_map/ppermute | solution.py:23
  40.5 1.4 %collective-permute-start.16 = (bf16[128,512]{1,0:T(8,128)(2,1)S(1)}, bf16[128,512]{1,0:T(8,128)(2,1)S(1)}, u32[]{:S(2)}, u32[]{:S(2)}) collective-permute-start(bf16[128,512]{1,0:T(8,128)(2,1)S(1)} %fusion.8), channel_id=1, source_target_pairs={{14,22},{15,23}} | collective-permute-start | bytes 393224 | tf_op jit(solution)/shard_map/ppermute | solution.py:23
  41.2 0.7 collective-permute-start.15
  42.3 1.4 %collective-permute-start.18 = (bf16[128,512]{1,0:T(8,128)(2,1)S(1)}, bf16[128,512]{1,0:T(8,128)(2,1)S(1)}, u32[]{:S(2)}, u32[]{:S(2)}) collective-permute-start(bf16[128,512]{1,0:T(8,128)(2,1)S(1)} %fusion.9), channel_id=1, source_target_pairs={{6,10},{22,26},{7,11},{23,27}} | collective-permute-start | bytes 393224 | tf_op jit(solution)/shard_map/ppermute | solution.py:23
  43.0 0.7 collective-permute-start.17
  44.2 2.7 %collective-permute-start.20 = (bf16[128,512]{1,0:T(8,128)(2,1)S(1)}, bf16[128,512]{1,0:T(8,128)(2,1)S(1)}, u32[]{:S(2)}, u32[]{:S(2)}) collective-permute-start(bf16[128,512]{1,0:T(8,128)(2,1)S(1)} %fusion.10), channel_id=1, source_target_pairs={{2,4},{10,12},{18,20},{26,28},{3,5},{11,13},{19,21},{27,29}} | collective-permute-start | bytes 393224 | tf_op jit(solution)/shard_map/ppermute | solution.py:23
  44.8 28.4 %collective-permute-start.19 = (bf16[128,512]{1,0:T(8,128)(2,1)S(1)}, bf16[128,512]{1,0:T(8,128)(2,1)S(1)}, u32[]{:S(2)}, u32[]{:S(2)}) collective-permute-start(bf16[128,512]{1,0:T(8,128)(2,1)S(1)} %fusion.10), channel_id=1, source_target_pairs={{2,0},{10,8},{18,16},{26,24},{3,1},{11,9},{19,17},{27,25}} | collective-permute-start | bytes 393224 | tf_op jit(solution)/shard_map/ppermute | solution.py:23
  46.2 27.6 %collective-permute-start.24 = (f32[128,512]{1,0:T(8,128)S(1)}, f32[128,512]{1,0:T(8,128)S(1)}, u32[]{:S(2)}, u32[]{:S(2)}) collective-permute-start(f32[128,512]{1,0:T(8,128)S(1)} %fusion.53), channel_id=1, source_target_pairs={{14,30},{15,31}} | collective-permute-start | bytes 786440 | tf_op jit(solution)/shard_map/ppermute | solution.py:108
  73.8 4.0 %collective-permute-start.21 = (bf16[128,512]{1,0:T(8,128)(2,1)S(1)}, bf16[128,512]{1,0:T(8,128)(2,1)S(1)}, u32[]{:S(2)}, u32[]{:S(2)}) collective-permute-start(bf16[128,512]{1,0:T(8,128)(2,1)S(1)} %get-tuple-element.7), channel_id=1, source_target_pairs={{0,2},{4,6},{8,10},{12,14},{16,18},{20,22},{24,26},{28,30},{1,3},{... | collective-permute-start | bytes 393224 | tf_op jit(solution)/shard_map/ppermute | solution.py:94
  77.8 1.5 %collective-permute-start.22 = (bf16[128,512]{1,0:T(8,128)(2,1)S(1)}, bf16[128,512]{1,0:T(8,128)(2,1)}, u32[]{:S(2)}, u32[]{:S(2)}) collective-permute-start(bf16[128,512]{1,0:T(8,128)(2,1)S(1)} %broadcast_select_fusion.1), channel_id=1, source_target_pairs={{0,1},{1,0},{2,3},{3,2},{4,5},{5,4},{6,7},{7,6},{8,9},{9,8},{10,11... | collective-permute-start | bytes 393224 | tf_op jit(solution)/shard_map/ppermute | solution.py:19
  84.4 3.8 %collective-permute-start.23 = (f32[256,1024]{1,0:T(8,128)}, f32[256,1024]{1,0:T(8,128)}, u32[]{:S(2)}, u32[]{:S(2)}) collective-permute-start(f32[256,1024]{1,0:T(8,128)} %constant_dynamic-slice_fusion.1), channel_id=1, source_target_pairs={{0,1},{1,0},{2,3},{3,2},{4,5},{5,4},{6,7},{7,6},{8,9},{9,8},{10,11... | collective-permute-start | bytes 3145736 | tf_op jit(solution)/shard_map/ppermute | solution.py:19
  85.3 2.2 %collective-permute-start.25 = (f32[128,256]{1,0:T(8,128)}, f32[128,256]{1,0:T(8,128)S(1)}, u32[]{:S(2)}, u32[]{:S(2)}) collective-permute-start(f32[128,256]{1,0:T(8,128)} %get-tuple-element.5), channel_id=1, source_target_pairs={{0,1},{1,0},{2,3},{3,2},{4,5},{5,4},{6,7},{7,6},{8,9},{9,8},{10,11... | collective-permute-start | bytes 393224 | tf_op jit(solution)/shard_map/ppermute | solution.py:19

commit v2 on v1

v2 whole, which is shorter than its diff:
```python
import jax
import jax.numpy as jnp
from jax import lax
from jax.sharding import PartitionSpec as P


ROWS = (((1,), (0,)), ((), ()))
BOTH = (((1,), (1,)), ((), ()))
FIRST = (((0,), (0,)), ((), ()))


def product(left, right, dims, precision=lax.Precision.HIGH):
    return lax.dot_general(
        left, right, dims, precision=precision, preferred_element_type=jnp.float32
    )


def swap(value):
    pairs = [(source, source ^ 1) for source in range(lax.axis_size("sep"))]
    return lax.ppermute(value, "sep", pairs)


def send(value, pairs):
    return lax.ppermute(value.astype(jnp.bfloat16), "leaf", pairs).astype(jnp.float32)


def join(mine, other, first, axis):
    return jnp.where(
        first,
        jnp.concatenate([mine, other], axis=axis),
        jnp.concatenate([other, mine], axis=axis),
    )


def columns(value, which, wide):
    return lax.dynamic_slice_in_dim(value, which * wide, wide, 1)


def solve(leaf_rhs, leaf_inv, leaf_couple, sep_rhs, sep_inv, sep_couple):
    count = lax.axis_size("leaf")
    depth = count.bit_length() - 1
    place = lax.axis_index("leaf")
    core = lax.axis_index("sep")
    first = core == 0
    even = place % 2 == 0
    inv_rows = leaf_inv[0]
    couple_cols = leaf_couple[0]
    half = leaf_rhs.shape[1] // 2
    half_sep = sep_rhs.shape[2]
    top, below = count - 1, count // 2 - 1

    def my_rows(value):
        return lax.dynamic_slice_in_dim(value, core * half, half, 0)

    def other_rows(value):
        return lax.dynamic_slice_in_dim(value, (1 - core) * half, half, 0)

    wide = leaf_rhs.shape[2]
    inv_half, couple_half, sep_local = sep_inv[0], sep_couple[0], sep_rhs[0]
    rhs_own = leaf_rhs[0]
    rhs_other = swap(rhs_own)
    top_half = lax.ppermute(inv_half, "leaf", [(top, below)])
    near = product(rhs_own, columns(inv_rows, core, wide), BOTH, None)
    far = product(rhs_other, columns(inv_rows, 1 - core, wide), BOTH, None)
    leaf_state = (near + far).astype(jnp.bfloat16)
    theirs = product(other_rows(leaf_state), couple_cols, BOTH, None)
    ours = product(my_rows(leaf_state), couple_cols, BOTH, None)

    rhs_rows = join(my_rows(sep_local), swap(other_rows(sep_local)), first, 1)

    def both_cores(part):
        return part + swap(part)

    outgoing = ours + swap(theirs)
    couple_late, inv_late, _ = lax.optimization_barrier((couple_half, inv_half, leaf_state))
    pull = both_cores(product(couple_late, inv_late, ROWS))
    work = rhs_rows - jnp.where(even, outgoing, 0.0)
    work = work - send(outgoing, [(k + 1, k) for k in range(0, count, 2)])
    for level in range(1, depth):
        reach = 2 ** (level - 1)
        parents = range(2 * reach - 1, count, 4 * reach)
        outgoing = product(work, pull, BOTH)
        lower = send(outgoing, [(k - reach, k) for k in parents])
        upper = send(outgoing, [(k + reach, k) for k in parents])
        if level == 1:
            inv_late, rhs_late, _ = lax.optimization_barrier((inv_half, rhs_rows, outgoing))
            gram = both_cores(product(inv_late, inv_late, FIRST))
            top_rhs = lax.ppermute(rhs_late, "leaf", [(top, below)])
        if level == 2:
            top_late, _ = lax.optimization_barrier((top_half, outgoing))
            top_gram = both_cores(product(top_late, top_late, FIRST))
        work = work - (lower + upper)
    top_work = top_rhs - product(work, pull, BOTH)
    top_solution = product(top_work, top_gram, ROWS)
    parent = top_solution
    state = product(work, gram, ROWS)
    for level in range(depth, 1, -1):
        reach = 2 ** (level - 2)
        slots = range(2 * reach - 1, count, 4 * reach)
        solved = state - product(parent, pull, ROWS)
        lower = send(solved, [(k, k - reach) for k in slots])
        upper = send(solved, [(k, k + reach) for k in slots])
        if level == 2:
            top_late, _ = lax.optimization_barrier((top_solution, solved))
            from_below = lax.ppermute(top_late, "leaf", [(below, top)])
        parent = parent + (lower + upper)
    solved = state - product(parent, pull, ROWS)
    narrow = solved.astype(jnp.bfloat16)
    beside = lax.ppermute(narrow, "leaf", [(k, k + 1) for k in range(0, count, 2)])
    parent_rows = jnp.where(even, narrow, beside)

    parent_full = join(parent_rows, swap(parent_rows), first, 0)
    pulled = jnp.dot(parent_full, couple_cols, preferred_element_type=jnp.float32)
    residue = (leaf_state.astype(jnp.float32) - pulled).astype(jnp.bfloat16)
    away = product(residue, columns(inv_rows, 1 - core, wide), ROWS, None)
    arrived = swap(away)
    here = product(residue, columns(inv_rows, core, wide), ROWS, None)
    leaf_solution = here + arrived

    solved_late, from_below, _ = lax.optimization_barrier((solved, from_below, parent_rows))
    whole = jnp.where(place == top, from_below, solved_late)
    sep_solution = join(
        columns(whole, core, half_sep), swap(columns(whole, 1 - core, half_sep)), first, 0
    )
    return (leaf_solution[None], sep_solution[None])


def solution(mesh):
    return jax.shard_map(
        solve,
        mesh=mesh,
        in_specs=(
            P("leaf", None, "sep"),
            P("leaf", "sep", None),
            P("leaf", None, "sep"),
            P("leaf", None, "sep"),
            P("leaf", "sep", None),
            P("leaf", None, "sep"),
        ),
        out_specs=(P("leaf", None, "sep"), P("leaf", None, "sep")),
        check_vma=False,
    )
```

time: 91 us -> 96.3 us (1.058)
  the two profiles are of different devices: /device:TPU:0 before, /device:TPU:31 now
where the time goes in v2:
time: 96.3 us; the launch traced here: 95.8 us
  waiting for transfers between devices  38.4 us (40%)
  starting transfers between devices  28.8 us (30%)
  matrix products  23.4 us (24%)
  other arithmetic  3.38 us (4%)
  between operations  1.07 us (1%)
    ppermute x1, waiting for transfers between devices, solve(): lax.ppermute(narrow, 'leaf', [(k, k + 1) for k in range(0, count, 2)])  26.4 us
    dot_general x19, matrix products, product(): lax.dot_general(left, right, dims, precision=precision, preferred_element...  22.9 us
    ppermute x13, starting transfers between devices, send(): lax.ppermute(value.astype(jnp.bfloat16), 'leaf', pairs).astype(jnp.float32)  11.1 us
    ppermute x9, starting transfers between devices, swap(): return lax.ppermute(value, 'sep', pairs)  11 us
    ppermute x1, waiting for transfers between devices, solve(): from_below = lax.ppermute(top_late, 'leaf', [(below, top)])  9.21 us
    ppermute x1, starting transfers between devices, solve(): top_half = lax.ppermute(inv_half, 'leaf', [(top, below)])  2.75 us
    ppermute x9, waiting for transfers between devices, swap(): return lax.ppermute(value, 'sep', pairs)  2.74 us
  transfers between devices with their start and end apart: 26, of which 5 were waited for; matrix products, arithmetic and copies ran while one was open for 21% of the time, Pallas kernels for 0%

profile of v2, /device:TPU:31, one launch (start us, length us, event | category | flops | bytes accessed | tf_op | source)
XLA Modules:
  0.0 95.8 jit_solution(5623592741712489930)
XLA Ops:
  0.6 0.7 collective-permute-start
  1.4 1.8 %fusion.60 = f32[512,512]{1,0:T(8,128)S(1)} fusion(f32[512,256]{1,0:T(8,128)} %bitcast.69, f32[256,512]{1,0:T(8,128)} %bitcast.66), kind=kOutput, calls=%fused_computation.73 | convolution fusion | flops 402653184 | bytes 2097152 | tf_op jit(solution)/shard_map/dot_general | solution.py:13
  3.3 2.5 %fusion.6 = f32[1024,256]{1,0:T(8,128)S(1)} fusion(bf16[1,1024,2048]{2,1,0:T(8,128)(2,1)} %param.7, s32[]{:T(128)S(6)} %select_n.80, bf16[1,256,1024]{2,1,0:T(8,128)(2,1)} %param.6), kind=kOutput, calls=%fused_computation.6 | convolution fusion | flops 536870912 | bytes 3670020 | tf_op jit(solution)/shard_map/dot_general | solution.py:13
  5.8 2.5 %fusion.21 = bf16[1024,256]{1,0:T(8,128)(2,1)S(1)} fusion(f32[1024,256]{1,0:T(8,128)S(1)} %fusion.6, bf16[256,1024]{1,0:T(8,128)(2,1)} %collective-permute-done, bf16[1,1024,2048]{2,1,0:T(8,128)(2,1)} %param.7, s32[]{:T(128)S(6)} %select_n.81), kind=kOutput, calls=%fused_computation.15 | convolution fusion | flops 537395200 | bytes 4194308 | tf_op jit(solution)/shard_map/dot_general | solution.py:13
  8.4 1.2 %fusion.28 = f32[128,512]{1,0:T(8,128)} fusion(bf16[1,512,1024]{2,1,0:T(8,128)(2,1)S(1)} %copy-done, bf16[1024,256]{1,0:T(8,128)(2,1)S(1)} %fusion.21, s32[]{:T(128)S(6)} %select_n.87), kind=kOutput, calls=%fused_computation.27 | convolution fusion | flops 134217728 | bytes 1572868 | tf_op jit(solution)/shard_map/dot_general | solution.py:13
  10.0 0.7 dynamic-slice_bitcast_fusion.1
  10.7 0.8 collective-permute-done.2
  11.5 2.1 %fusion.58 = (bf16[128,512]{1,0:T(8,128)(2,1)}, f32[128,512]{1,0:T(8,128)S(1)}) fusion(f32[128,512]{1,0:T(8,128)} %collective-permute-done.2, bf16[1,512,1024]{2,1,0:T(8,128)(2,1)S(1)} %copy-done, bf16[1024,256]{1,0:T(8,128)(2,1)S(1)} %fusion.21, s32[]{:T(128)S(6)} %select_n.86), kind=kOutput, calls=%fused_computation.71 | convolution fusion | flops 134348800 | bytes 1966084 | tf_op jit(solution)/shard_map/dot_general | solution.py:13
  13.6 2.8 %collective-permute-start.3 = (bf16[128,512]{1,0:T(8,128)(2,1)}, bf16[128,512]{1,0:T(8,128)(2,1)}, u32[]{:S(2)}, u32[]{:S(2)}) collective-permute-start(bf16[128,512]{1,0:T(8,128)(2,1)} %get-tuple-element.24), channel_id=1, source_target_pairs={{2,0},{6,4},{10,8},{14,12},{18,16},{22,20},{26,24},{30,28},{3,1},{... | collective-permute-start | bytes 393224 | tf_op jit(solution)/shard_map/ppermute | solution.py:24
  16.4 2.8 %collective-permute-start.13 = (f32[256,512]{1,0:T(8,128)S(1)}, f32[256,512]{1,0:T(8,128)}, u32[]{:S(2)}, u32[]{:S(2)}) collective-permute-start(f32[256,512]{1,0:T(8,128)S(1)} %bitcast.67), channel_id=1, source_target_pairs={{30,14},{31,15}} | collective-permute-start | bytes 1572872 | tf_op jit(solution)/shard_map/ppermute | solution.py:62
  19.2 1.1 %convert_subtract_fusion = (f32[128,512]{1,0:T(8,128)S(1)}, f32[128,512]{1,0:T(8,128)S(1)}) fusion(bf16[128,512]{1,0:T(8,128)(2,1)} %collective-permute-done.3, f32[128,512]{1,0:T(8,128)S(1)} %get-tuple-element.25, pred[]{:T(512)S(6)} %eq.12, f32[128,256]{1,0:T(8,128)S(1)} %get-tuple-element.23, f32[128,256]{1,0:T(8,128)} %collective-permute-done.1, pred[]{:T(512)S(6)} %eq.11), kind=kLoop, calls=%fused_computation.52 | loop fusion | flops 458752 | bytes 1179650 | tf_op jit(solution)/shard_map/sub | solution.py:78
  20.3 1.4 %add.79 = f32[512,512]{1,0:T(8,128)S(1)} add(f32[512,512]{1,0:T(8,128)S(1)} %fusion.60, f32[512,512]{1,0:T(8,128)} %collective-permute-done.4) | non-fusion elementwise | flops 262144 | bytes 3145728 | tf_op jit(solution)/shard_map/add | solution.py:72
  21.7 0.7 fusion.61
  22.4 0.7 collective-permute-start.5
  23.1 0.7 collective-permute-start.6
  23.7 1.3 %collective-permute-start.12 = (f32[128,512]{1,0:T(8,128)S(1)}, f32[128,512]{1,0:T(8,128)S(1)}, u32[]{:S(2)}, u32[]{:S(2)}) collective-permute-start(f32[128,512]{1,0:T(8,128)S(1)} %get-tuple-element.13), channel_id=1, source_target_pairs={{30,14},{31,15}} | collective-permute-start | bytes 786440 | tf_op jit(solution)/shard_map/ppermute | solution.py:88
  25.1 0.6 fusion.62
  25.7 1.6 %collective-permute-start.11 = (f32[512,512]{1,0:T(8,128)S(1)}, f32[512,512]{1,0:T(8,128)S(1)}, u32[]{:S(2)}, u32[]{:S(2)}) collective-permute-start(f32[512,512]{1,0:T(8,128)S(1)} %fusion.62), channel_id=1, source_target_pairs={{0,1},{1,0},{2,3},{3,2},{4,5},{5,4},{6,7},{7,6},{8,9},{9,8},{10,11... | collective-permute-start | bytes 3145736 | tf_op jit(solution)/shard_map/ppermute | solution.py:20
  27.3 0.7 fusion.49
  28.0 0.7 collective-permute-start.7
  28.7 0.7 collective-permute-start.8
  29.3 1.8 %fusion.63 = f32[512,512]{1,0:T(8,128)S(1)} fusion(f32[256,512]{1,0:T(8,128)} %collective-permute-done.13), kind=kOutput, calls=%fused_computation.76 | convolution fusion | flops 402653184 | bytes 1572864 | tf_op jit(solution)/shard_map/dot_general | solution.py:13
  31.2 2.3 %collective-permute-start.14 = (f32[512,512]{1,0:T(8,128)S(1)}, f32[512,512]{1,0:T(8,128)S(1)}, u32[]{:S(2)}, u32[]{:S(2)}) collective-permute-start(f32[512,512]{1,0:T(8,128)S(1)} %fusion.63), channel_id=1, source_target_pairs={{0,1},{1,0},{2,3},{3,2},{4,5},{5,4},{6,7},{7,6},{8,9},{9,8},{10,11... | collective-permute-start | bytes 3145736 | tf_op jit(solution)/shard_map/ppermute | solution.py:20
  33.6 0.7 convolution_convert_fusion
  34.3 0.7 collective-permute-start.10
  34.9 0.7 collective-permute-start.9
  35.6 0.7 convolution_subtract_fusion.4
  36.3 0.5 fusion.33
  37.7 0.7 collective-permute-start.15
  38.3 0.7 collective-permute-start.16
  39.5 0.8 collective-permute-start.17
  40.3 0.8 collective-permute-start.18
  41.1 0.5 convolution_subtract_fusion.1
  41.6 0.7 collective-permute-start.19
  42.3 0.7 collective-permute-start.20
  43.0 0.5 fusion.59
  43.5 1.3 %collective-permute-start.21 = (bf16[128,512]{1,0:T(8,128)(2,1)S(1)}, bf16[128,512]{1,0:T(8,128)(2,1)S(1)}, u32[]{:S(2)}, u32[]{:S(2)}) collective-permute-start(bf16[128,512]{1,0:T(8,128)(2,1)S(1)} %get-tuple-element.26), channel_id=1, source_target_pairs={{0,2},{4,6},{8,10},{12,14},{16,18},{20,22},{24,26},{28,30},{1,3},{... | collective-permute-start | bytes 393224 | tf_op jit(solution)/shard_map/ppermute | solution.py:109
  44.8 26.4 %collective-permute-done.21 = bf16[128,512]{1,0:T(8,128)(2,1)S(1)} collective-permute-done((bf16[128,512]{1,0:T(8,128)(2,1)S(1)}, bf16[128,512]{1,0:T(8,128)(2,1)S(1)}, u32[]{:S(2)}, u32[]{:S(2)}) %collective-permute-start.21) | collective-permute-done | bytes 131104 | tf_op jit(solution)/shard_map/ppermute | solution.py:109
  71.2 4.3 %collective-permute-start.22 = (bf16[128,512]{1,0:T(8,128)(2,1)S(1)}, bf16[128,512]{1,0:T(8,128)(2,1)S(1)}, u32[]{:S(2)}, u32[]{:S(2)}) collective-permute-start(bf16[128,512]{1,0:T(8,128)(2,1)S(1)} %broadcast_select_fusion.1), channel_id=1, source_target_pairs={{0,1},{1,0},{2,3},{3,2},{4,5},{5,4},{6,7},{7,6},{8,9},{9,8},{10,11... | collective-permute-start | bytes 393224 | tf_op jit(solution)/shard_map/ppermute | solution.py:20
  75.5 1.0 %collective-permute-done.22 = bf16[128,512]{1,0:T(8,128)(2,1)S(1)} collective-permute-done((bf16[128,512]{1,0:T(8,128)(2,1)S(1)}, bf16[128,512]{1,0:T(8,128)(2,1)S(1)}, u32[]{:S(2)}, u32[]{:S(2)}) %collective-permute-start.22) | collective-permute-done | bytes 131104 | tf_op jit(solution)/shard_map/ppermute | solution.py:20
  76.5 0.6 subtract_convert_fusion
  77.0 1.7 %fusion = f32[256,1024]{1,0:T(8,128)} fusion(bf16[256,1024]{0,1:T(8,128)(2,1)S(1)} %subtract_convert_fusion, bf16[1,1024,2048]{2,1,0:T(8,128)(2,1)S(1)} %copy-done.1, s32[]{:T(128)S(6)} %select_n.81), kind=kOutput, calls=%fused_computation | convolution fusion | flops 536870912 | bytes 3670020 | tf_op jit(solution)/shard_map/dot_general | solution.py:13
  79.1 1.3 %collective-permute-start.24 = (f32[128,512]{1,0:T(8,128)S(1)}, f32[128,512]{1,0:T(8,128)S(1)}, u32[]{:S(2)}, u32[]{:S(2)}) collective-permute-start(f32[128,512]{1,0:T(8,128)S(1)} %fusion.31), channel_id=1, source_target_pairs={{14,30},{15,31}} | collective-permute-start | bytes 786440 | tf_op jit(solution)/shard_map/ppermute | solution.py:105
  80.4 9.2 %collective-permute-done.24 = f32[128,512]{1,0:T(8,128)S(1)} collective-permute-done((f32[128,512]{1,0:T(8,128)S(1)}, f32[128,512]{1,0:T(8,128)S(1)}, u32[]{:S(2)}, u32[]{:S(2)}) %collective-permute-start.24) | collective-permute-done | bytes 262176 | tf_op jit(solution)/shard_map/ppermute | solution.py:105
  89.7 1.1 %collective-permute-start.25 = (f32[128,256]{1,0:T(8,128)S(1)}, f32[128,256]{1,0:T(8,128)S(1)}, u32[]{:S(2)}, u32[]{:S(2)}) collective-permute-start(f32[128,256]{1,0:T(8,128)S(1)} %get-tuple-element.21), channel_id=1, source_target_pairs={{0,1},{1,0},{2,3},{3,2},{4,5},{5,4},{6,7},{7,6},{8,9},{9,8},{10,11... | collective-permute-start | bytes 393224 | tf_op jit(solution)/shard_map/ppermute | solution.py:20
  90.8 1.0 %collective-permute-done.25 = f32[128,256]{1,0:T(8,128)S(1)} collective-permute-done((f32[128,256]{1,0:T(8,128)S(1)}, f32[128,256]{1,0:T(8,128)S(1)}, u32[]{:S(2)}, u32[]{:S(2)}) %collective-permute-start.25) | collective-permute-done | bytes 131104 | tf_op jit(solution)/shard_map/ppermute | solution.py:20
  91.8 0.7 maximum_select_fusion.5
  92.5 3.3 %fusion.15 = f32[1,256,1024]{2,1,0:T(8,128)} fusion(f32[256,1024]{1,0:T(8,128)S(1)} %collective-permute-done.23, bf16[256,1024]{0,1:T(8,128)(2,1)S(1)} %subtract_convert_fusion, bf16[1,1024,2048]{2,1,0:T(8,128)(2,1)} %param.7, s32[]{:T(128)S(6)} %select_n.80), kind=kOutput, calls=%fused_computation.13 | convolution fusion | flops 537133056 | bytes 4718596 | tf_op jit(solution)/shard_map/dot_general | solution.py:13
  (40 shorter events, 2.5 us)
Async XLA Ops:
  0.6 7.7 %copy-start = (bf16[1,512,1024]{2,1,0:T(8,128)(2,1)S(1)}, bf16[1,512,1024]{2,1,0:T(8,128)(2,1)}, u32[]{:S(2)}) copy-start(bf16[1,512,1024]{2,1,0:T(8,128)(2,1)} %param.8) | copy-start | bytes 3145732
  0.6 5.2 %collective-permute-start = (bf16[256,1024]{1,0:T(8,128)(2,1)}, bf16[256,1024]{1,0:T(8,128)(2,1)}, u32[]{:S(2)}, u32[]{:S(2)}) collective-permute-start(bf16[256,1024]{1,0:T(8,128)(2,1)} %bitcast.70), channel_id=1, source_target_pairs={{0,1},{1,0},{2,3},{3,2},{4,5},{5,4},{6,7},{7,6},{8,9},{9,8},{10,11... | collective-permute-start | bytes 1572872 | tf_op jit(solution)/shard_map/ppermute | solution.py:20
  3.2 17.1 %collective-permute-start.4 = (f32[512,512]{1,0:T(8,128)S(1)}, f32[512,512]{1,0:T(8,128)}, u32[]{:S(2)}, u32[]{:S(2)}) collective-permute-start(f32[512,512]{1,0:T(8,128)S(1)} %fusion.60), channel_id=1, source_target_pairs={{0,1},{1,0},{2,3},{3,2},{4,5},{5,4},{6,7},{7,6},{8,9},{9,8},{10,11... | collective-permute-start | bytes 3145736 | tf_op jit(solution)/shard_map/ppermute | solution.py:20
  3.3 6.7 %copy-start.3 = (f32[1,256,256]{2,1,0:T(8,128)S(1)}, f32[1,256,256]{2,1,0:T(8,128)}, u32[]{:S(2)}) copy-start(f32[1,256,256]{2,1,0:T(8,128)} %param.9) | copy-start | bytes 786436
  5.8 10.6 %copy-start.2 = (f32[1,256,512]{2,1,0:T(8,128)S(1)}, f32[1,256,512]{2,1,0:T(8,128)}, u32[]{:S(2)}) copy-start(f32[1,256,512]{2,1,0:T(8,128)} %param.10) | copy-start | bytes 1572868
  9.6 1.9 %collective-permute-start.2 = (f32[128,512]{1,0:T(8,128)}, f32[128,512]{1,0:T(8,128)}, u32[]{:S(2)}, u32[]{:S(2)}) collective-permute-start(f32[128,512]{1,0:T(8,128)} %fusion.28), channel_id=1, source_target_pairs={{0,1},{1,0},{2,3},{3,2},{4,5},{5,4},{6,7},{7,6},{8,9},{9,8},{10,11... | collective-permute-start | bytes 786440 | tf_op jit(solution)/shard_map/ppermute | solution.py:20
  10.7 8.5 %collective-permute-start.1 = (f32[128,256]{1,0:T(8,128)}, f32[128,256]{1,0:T(8,128)}, u32[]{:S(2)}, u32[]{:S(2)}) collective-permute-start(f32[128,256]{1,0:T(8,128)} %get-tuple-element.22), channel_id=1, source_target_pairs={{0,1},{1,0},{2,3},{3,2},{4,5},{5,4},{6,7},{7,6},{8,9},{9,8},{10,11... | collective-permute-start | bytes 393224 | tf_op jit(solution)/shard_map/ppermute | solution.py:20
  13.6 5.6 %collective-permute-start.3 = (bf16[128,512]{1,0:T(8,128)(2,1)}, bf16[128,512]{1,0:T(8,128)(2,1)}, u32[]{:S(2)}, u32[]{:S(2)}) collective-permute-start(bf16[128,512]{1,0:T(8,128)(2,1)} %get-tuple-element.24), channel_id=1, source_target_pairs={{2,0},{6,4},{10,8},{14,12},{18,16},{22,20},{26,24},{30,28},{3,1},{... | collective-permute-start | bytes 393224 | tf_op jit(solution)/shard_map/ppermute | solution.py:24
  16.4 12.9 %collective-permute-start.13 = (f32[256,512]{1,0:T(8,128)S(1)}, f32[256,512]{1,0:T(8,128)}, u32[]{:S(2)}, u32[]{:S(2)}) collective-permute-start(f32[256,512]{1,0:T(8,128)S(1)} %bitcast.67), channel_id=1, source_target_pairs={{30,14},{31,15}} | collective-permute-start | bytes 1572872 | tf_op jit(solution)/shard_map/ppermute | solution.py:62
  22.4 4.9 %collective-permute-start.5 = (bf16[128,512]{1,0:T(8,128)(2,1)S(1)}, bf16[128,512]{1,0:T(8,128)(2,1)S(1)}, u32[]{:S(2)}, u32[]{:S(2)}) collective-permute-start(bf16[128,512]{1,0:T(8,128)(2,1)S(1)} %fusion.61), channel_id=1, source_target_pairs={{0,2},{8,10},{16,18},{24,26},{1,3},{9,11},{17,19},{25,27}} | collective-permute-start | bytes 393224 | tf_op jit(solution)/shard_map/ppermute | solution.py:24
  23.1 4.2 %collective-permute-start.6 = (bf16[128,512]{1,0:T(8,128)(2,1)S(1)}, bf16[128,512]{1,0:T(8,128)(2,1)S(1)}, u32[]{:S(2)}, u32[]{:S(2)}) collective-permute-start(bf16[128,512]{1,0:T(8,128)(2,1)S(1)} %fusion.61), channel_id=1, source_target_pairs={{4,2},{12,10},{20,18},{28,26},{5,3},{13,11},{21,19},{29,27}} | collective-permute-start | bytes 393224 | tf_op jit(solution)/shard_map/ppermute | solution.py:24
  23.7 11.9 %collective-permute-start.12 = (f32[128,512]{1,0:T(8,128)S(1)}, f32[128,512]{1,0:T(8,128)S(1)}, u32[]{:S(2)}, u32[]{:S(2)}) collective-permute-start(f32[128,512]{1,0:T(8,128)S(1)} %get-tuple-element.13), channel_id=1, source_target_pairs={{30,14},{31,15}} | collective-permute-start | bytes 786440 | tf_op jit(solution)/shard_map/ppermute | solution.py:88
  25.7 10.6 %collective-permute-start.11 = (f32[512,512]{1,0:T(8,128)S(1)}, f32[512,512]{1,0:T(8,128)S(1)}, u32[]{:S(2)}, u32[]{:S(2)}) collective-permute-start(f32[512,512]{1,0:T(8,128)S(1)} %fusion.62), channel_id=1, source_target_pairs={{0,1},{1,0},{2,3},{3,2},{4,5},{5,4},{6,7},{7,6},{8,9},{9,8},{10,11... | collective-permute-start | bytes 3145736 | tf_op jit(solution)/shard_map/ppermute | solution.py:20
  28.0 5.5 %collective-permute-start.7 = (bf16[128,512]{1,0:T(8,128)(2,1)S(1)}, bf16[128,512]{1,0:T(8,128)(2,1)S(1)}, u32[]{:S(2)}, u32[]{:S(2)}) collective-permute-start(bf16[128,512]{1,0:T(8,128)(2,1)S(1)} %fusion.49), channel_id=1, source_target_pairs={{2,6},{18,22},{3,7},{19,23}} | collective-permute-start | bytes 393224 | tf_op jit(solution)/shard_map/ppermute | solution.py:24
  28.7 4.9 %collective-permute-start.8 = (bf16[128,512]{1,0:T(8,128)(2,1)S(1)}, bf16[128,512]{1,0:T(8,128)(2,1)S(1)}, u32[]{:S(2)}, u32[]{:S(2)}) collective-permute-start(bf16[128,512]{1,0:T(8,128)(2,1)S(1)} %fusion.49), channel_id=1, source_target_pairs={{10,6},{26,22},{11,7},{27,23}} | collective-permute-start | bytes 393224 | tf_op jit(solution)/shard_map/ppermute | solution.py:24
  31.2 5.6 %collective-permute-start.14 = (f32[512,512]{1,0:T(8,128)S(1)}, f32[512,512]{1,0:T(8,128)S(1)}, u32[]{:S(2)}, u32[]{:S(2)}) collective-permute-start(f32[512,512]{1,0:T(8,128)S(1)} %fusion.63), channel_id=1, source_target_pairs={{0,1},{1,0},{2,3},{3,2},{4,5},{5,4},{6,7},{7,6},{8,9},{9,8},{10,11... | collective-permute-start | bytes 3145736 | tf_op jit(solution)/shard_map/ppermute | solution.py:20
  34.3 1.4 %collective-permute-start.10 = (bf16[128,512]{1,0:T(8,128)(2,1)S(1)}, bf16[128,512]{1,0:T(8,128)(2,1)S(1)}, u32[]{:S(2)}, u32[]{:S(2)}) collective-permute-start(bf16[128,512]{1,0:T(8,128)(2,1)S(1)} %convolution_convert_fusion), channel_id=1, source_target_pairs={{22,14},{23,15}} | collective-permute-start | bytes 393224 | tf_op jit(solution)/shard_map/ppermute | solution.py:24
  34.9 0.7 collective-permute-start.9
  37.7 1.4 %collective-permute-start.15 = (bf16[128,512]{1,0:T(8,128)(2,1)S(1)}, bf16[128,512]{1,0:T(8,128)(2,1)S(1)}, u32[]{:S(2)}, u32[]{:S(2)}) collective-permute-start(bf16[128,512]{1,0:T(8,128)(2,1)S(1)} %fusion.24), channel_id=1, source_target_pairs={{14,6},{15,7}} | collective-permute-start | bytes 393224 | tf_op jit(solution)/shard_map/ppermute | solution.py:24
  38.3 0.7 collective-permute-start.16
  39.5 37.6 %copy-start.1 = (bf16[1,1024,2048]{2,1,0:T(8,128)(2,1)S(1)}, bf16[1,1024,2048]{2,1,0:T(8,128)(2,1)}, u32[]{:S(2)}) copy-start(bf16[1,1024,2048]{2,1,0:T(8,128)(2,1)} %param.7) | copy-start | bytes 12582916
  39.5 1.6 %collective-permute-start.17 = (bf16[128,512]{1,0:T(8,128)(2,1)S(1)}, bf16[128,512]{1,0:T(8,128)(2,1)S(1)}, u32[]{:S(2)}, u32[]{:S(2)}) collective-permute-start(bf16[128,512]{1,0:T(8,128)(2,1)S(1)} %fusion.25), channel_id=1, source_target_pairs={{6,2},{22,18},{7,3},{23,19}} | collective-permute-start | bytes 393224 | tf_op jit(solution)/shard_map/ppermute | solution.py:24
  40.3 0.8 collective-permute-start.18
  41.6 1.4 %collective-permute-start.19 = (bf16[128,512]{1,0:T(8,128)(2,1)S(1)}, bf16[128,512]{1,0:T(8,128)(2,1)S(1)}, u32[]{:S(2)}, u32[]{:S(2)}) collective-permute-start(bf16[128,512]{1,0:T(8,128)(2,1)S(1)} %convolution_subtract_fusion.1), channel_id=1, source_target_pairs={{2,0},{10,8},{18,16},{26,24},{3,1},{11,9},{19,17},{27,25}} | collective-permute-start | bytes 393224 | tf_op jit(solution)/shard_map/ppermute | solution.py:24
  42.3 0.7 collective-permute-start.20
  43.5 27.7 %collective-permute-start.21 = (bf16[128,512]{1,0:T(8,128)(2,1)S(1)}, bf16[128,512]{1,0:T(8,128)(2,1)S(1)}, u32[]{:S(2)}, u32[]{:S(2)}) collective-permute-start(bf16[128,512]{1,0:T(8,128)(2,1)S(1)} %get-tuple-element.26), channel_id=1, source_target_pairs={{0,2},{4,6},{8,10},{12,14},{16,18},{20,22},{24,26},{28,30},{1,3},{... | collective-permute-start | bytes 393224 | tf_op jit(solution)/shard_map/ppermute | solution.py:109
  71.2 5.3 %collective-permute-start.22 = (bf16[128,512]{1,0:T(8,128)(2,1)S(1)}, bf16[128,512]{1,0:T(8,128)(2,1)S(1)}, u32[]{:S(2)}, u32[]{:S(2)}) collective-permute-start(bf16[128,512]{1,0:T(8,128)(2,1)S(1)} %broadcast_select_fusion.1), channel_id=1, source_target_pairs={{0,1},{1,0},{2,3},{3,2},{4,5},{5,4},{6,7},{7,6},{8,9},{9,8},{10,11... | collective-permute-start | bytes 393224 | tf_op jit(solution)/shard_map/ppermute | solution.py:20
  78.8 13.7 %collective-permute-start.23 = (f32[256,1024]{1,0:T(8,128)}, f32[256,1024]{1,0:T(8,128)S(1)}, u32[]{:S(2)}, u32[]{:S(2)}) collective-permute-start(f32[256,1024]{1,0:T(8,128)} %fusion), channel_id=1, source_target_pairs={{0,1},{1,0},{2,3},{3,2},{4,5},{5,4},{6,7},{7,6},{8,9},{9,8},{10,11... | collective-permute-start | bytes 3145736 | tf_op jit(solution)/shard_map/ppermute | solution.py:20
  79.1 10.5 %collective-permute-start.24 = (f32[128,512]{1,0:T(8,128)S(1)}, f32[128,512]{1,0:T(8,128)S(1)}, u32[]{:S(2)}, u32[]{:S(2)}) collective-permute-start(f32[128,512]{1,0:T(8,128)S(1)} %fusion.31), channel_id=1, source_target_pairs={{14,30},{15,31}} | collective-permute-start | bytes 786440 | tf_op jit(solution)/shard_map/ppermute | solution.py:105
  89.7 2.1 %collective-permute-start.25 = (f32[128,256]{1,0:T(8,128)S(1)}, f32[128,256]{1,0:T(8,128)S(1)}, u32[]{:S(2)}, u32[]{:S(2)}) collective-permute-start(f32[128,256]{1,0:T(8,128)S(1)} %get-tuple-element.21), channel_id=1, source_target_pairs={{0,1},{1,0},{2,3},{3,2},{4,5},{5,4},{6,7},{7,6},{8,9},{9,8},{10,11... | collective-permute-start | bytes 393224 | tf_op jit(solution)/shard_map/ppermute | solution.py:20

commit v3 on v2

--- a/solution.py
+++ b/solution.py
@@ -60,9 +60,8 @@
     rhs_own = leaf_rhs[0]
     rhs_other = swap(rhs_own)
     top_half = lax.ppermute(inv_half, "leaf", [(top, below)])
-    near = product(rhs_own, columns(inv_rows, core, wide), BOTH, None)
-    far = product(rhs_other, columns(inv_rows, 1 - core, wide), BOTH, None)
-    leaf_state = (near + far).astype(jnp.bfloat16)
+    leaf_state = product(join(rhs_own, rhs_other, first, 1), inv_rows, BOTH, None)
+    leaf_state = leaf_state.astype(jnp.bfloat16)
     theirs = product(other_rows(leaf_state), couple_cols, BOTH, None)
     ours = product(my_rows(leaf_state), couple_cols, BOTH, None)
 
@@ -72,10 +71,11 @@
         return part + swap(part)
 
     outgoing = ours + swap(theirs)
-    couple_late, inv_late, _ = lax.optimization_barrier((couple_half, inv_half, leaf_state))
-    pull = both_cores(product(couple_late, inv_late, ROWS))
+    pull_part = product(couple_half, inv_half, ROWS)
+    pull = both_cores(pull_part)
     work = rhs_rows - jnp.where(even, outgoing, 0.0)
-    work = work - send(outgoing, [(k + 1, k) for k in range(0, count, 2)])
+    received = send(outgoing, [(k + 1, k) for k in range(0, count, 2)])
+    work = work - received
     for level in range(1, depth):
         reach = 2 ** (level - 1)
         parents = range(2 * reach - 1, count, 4 * reach)
@@ -100,14 +100,16 @@
         solved = state - product(parent, pull, ROWS)
         lower = send(solved, [(k, k - reach) for k in slots])
         upper = send(solved, [(k, k + reach) for k in slots])
-        if level == 2:
-            top_late, _ = lax.optimization_barrier((top_solution, solved))
-            from_below = lax.ppermute(top_late, "leaf", [(below, top)])
         parent = parent + (lower + upper)
     solved = state - product(parent, pull, ROWS)
-    narrow = solved.astype(jnp.bfloat16)
+    from_below = lax.ppermute(top_solution, "leaf", [(below, top)])
+    whole = jnp.where(place == top, from_below, solved)
+    narrow = whole.astype(jnp.bfloat16)
     beside = lax.ppermute(narrow, "leaf", [(k, k + 1) for k in range(0, count, 2)])
     parent_rows = jnp.where(even, narrow, beside)
+
+    whole_arrived = swap(columns(whole, 1 - core, half_sep))
+    sep_solution = join(columns(whole, core, half_sep), whole_arrived, first, 0)
 
     parent_full = join(parent_rows, swap(parent_rows), first, 0)
     pulled = jnp.dot(parent_full, couple_cols, preferred_element_type=jnp.float32)
@@ -117,11 +119,6 @@
     here = product(residue, columns(inv_rows, core, wide), ROWS, None)
     leaf_solution = here + arrived
 
-    solved_late, from_below, _ = lax.optimization_barrier((solved, from_below, parent_rows))
-    whole = jnp.where(place == top, from_below, solved_late)
-    sep_solution = join(
-        columns(whole, core, half_sep), swap(columns(whole, 1 - core, half_sep)), first, 0
-    )
     return (leaf_solution[None], sep_solution[None])
 
 

time: 96.3 us -> 90.3 us (0.938)
  the two profiles are of different devices: /device:TPU:31 before, /device:TPU:27 now
where the time goes in v3:
time: 90.3 us; the launch traced here: 89.7 us
  starting transfers between devices  34.2 us (38%)
  waiting for transfers between devices  26.4 us (29%)
  matrix products  23.7 us (26%)
  other arithmetic  3.7 us (4%)
  between operations  1.08 us (1%)
    dot_general x18, matrix products, product(): lax.dot_general(left, right, dims, precision=precision, preferred_element...  22.2 us
    ppermute x13, waiting for transfers between devices, send(): lax.ppermute(value.astype(jnp.bfloat16), 'leaf', pairs).astype(jnp.float32)  17.8 us
    ppermute x9, starting transfers between devices, swap(): return lax.ppermute(value, 'sep', pairs)  16.2 us
    ppermute x13, starting transfers between devices, send(): lax.ppermute(value.astype(jnp.bfloat16), 'leaf', pairs).astype(jnp.float32)  14.6 us
    ppermute x1, waiting for transfers between devices, solve(): lax.ppermute(narrow, 'leaf', [(k, k + 1) for k in range(0, count, 2)])  4.41 us
    ppermute x9, waiting for transfers between devices, swap(): return lax.ppermute(value, 'sep', pairs)  4.16 us
  transfers between devices with their start and end apart: 26, of which 9 were waited for; matrix products, arithmetic and copies ran while one was open for 20% of the time, Pallas kernels for 0%

profile of v3, /device:TPU:27, one launch (start us, length us, event | category | flops | bytes accessed | tf_op | source)
XLA Modules:
  0.0 89.7 jit_solution(1595949049064026603)
XLA Ops:
  0.7 0.7 collective-permute-start
  1.4 1.8 %fusion.35 = f32[512,512]{1,0:T(8,128)S(1)} fusion(f32[1,512,256]{2,1,0:T(8,128)} %param.11, f32[1,256,512]{2,1,0:T(8,128)} %param.10), kind=kOutput, calls=%fused_computation.38 | convolution fusion | flops 402653184 | bytes 2097152 | tf_op jit(solution)/shard_map/dot_general | solution.py:13
  3.4 4.0 %fusion.15 = bf16[256,1024]{1,0:T(8,128)(2,1)S(1)} fusion(bf16[1,1024,2048]{2,1,0:T(8,128)(2,1)} %param.7, bf16[256,1024]{1,0:T(8,128)(2,1)} %collective-permute-done, bf16[256,1024]{1,0:T(8,128)(2,1)S(1)} %bitcast.62, pred[]{:T(512)S(6)} %eq.11), kind=kOutput, calls=%fused_computation.12 | convolution fusion | flops 1078722560 | bytes 5767169 | tf_op jit(solution)/shard_map/dot_general | solution.py:13
  7.4 1.2 %fusion.27 = f32[128,512]{1,0:T(8,128)} fusion(bf16[1,512,1024]{2,1,0:T(8,128)(2,1)S(1)} %copy-done, bf16[256,1024]{1,0:T(8,128)(2,1)S(1)} %fusion.15, s32[]{:T(128)S(6)} %select_n.94), kind=kOutput, calls=%fused_computation.30 | convolution fusion | flops 134217728 | bytes 1572868 | tf_op jit(solution)/shard_map/dot_general | solution.py:13
  8.9 0.7 dynamic-slice_bitcast_fusion.1
  9.8 0.7 collective-permute-done.2
  10.5 2.1 %fusion.58 = (bf16[128,512]{1,0:T(8,128)(2,1)}, f32[128,512]{1,0:T(8,128)S(1)}) fusion(f32[128,512]{1,0:T(8,128)} %collective-permute-done.2, bf16[1,512,1024]{2,1,0:T(8,128)(2,1)S(1)} %copy-done, bf16[256,1024]{1,0:T(8,128)(2,1)S(1)} %fusion.15, s32[]{:T(128)S(6)} %select_n.93), kind=kOutput, calls=%fused_computation.76 | convolution fusion | flops 134348800 | bytes 1966084 | tf_op jit(solution)/shard_map/dot_general | solution.py:13
  12.6 2.8 %collective-permute-start.3 = (bf16[128,512]{1,0:T(8,128)(2,1)}, bf16[128,512]{1,0:T(8,128)(2,1)}, u32[]{:S(2)}, u32[]{:S(2)}) collective-permute-start(bf16[128,512]{1,0:T(8,128)(2,1)} %get-tuple-element.16), channel_id=1, source_target_pairs={{2,0},{6,4},{10,8},{14,12},{18,16},{22,20},{26,24},{30,28},{3,1},{... | collective-permute-start | bytes 393224 | tf_op jit(solution)/shard_map/ppermute | solution.py:24
  15.4 0.7 collective-permute-start.12
  16.1 1.5 %collective-permute-done.3 = bf16[128,512]{1,0:T(8,128)(2,1)} collective-permute-done((bf16[128,512]{1,0:T(8,128)(2,1)}, bf16[128,512]{1,0:T(8,128)(2,1)}, u32[]{:S(2)}, u32[]{:S(2)}) %collective-permute-start.3) | collective-permute-done | bytes 131104 | tf_op jit(solution)/shard_map/ppermute | solution.py:24
  17.7 1.1 %convert_subtract_fusion = (f32[128,512]{1,0:T(8,128)S(1)}, f32[128,512]{1,0:T(8,128)S(1)}) fusion(bf16[128,512]{1,0:T(8,128)(2,1)} %collective-permute-done.3, f32[128,512]{1,0:T(8,128)S(1)} %get-tuple-element.17, pred[]{:T(512)S(6)} %eq.12, f32[128,256]{1,0:T(8,128)S(1)} %get-tuple-element.15, f32[128,256]{1,0:T(8,128)} %collective-permute-done.1, pred[]{:T(512)S(6)} %eq.11), kind=kLoop, calls=%fused_computation.57 | loop fusion | flops 458752 | bytes 1179650 | tf_op jit(solution)/shard_map/sub | solution.py:78
  18.8 1.8 %add.70 = f32[512,512]{1,0:T(8,128)S(1)} add(f32[512,512]{1,0:T(8,128)} %copy-done.2, f32[512,512]{1,0:T(8,128)} %collective-permute-done.4) | non-fusion elementwise | flops 262144 | bytes 3145728 | tf_op jit(solution)/shard_map/add | solution.py:71
  20.5 0.7 fusion.59
  21.2 1.3 %collective-permute-start.7 = (bf16[128,512]{1,0:T(8,128)(2,1)S(1)}, bf16[128,512]{1,0:T(8,128)(2,1)S(1)}, u32[]{:S(2)}, u32[]{:S(2)}) collective-permute-start(bf16[128,512]{1,0:T(8,128)(2,1)S(1)} %fusion.59), channel_id=1, source_target_pairs={{4,2},{12,10},{20,18},{28,26},{5,3},{13,11},{21,19},{29,27}} | collective-permute-start | bytes 393224 | tf_op jit(solution)/shard_map/ppermute | solution.py:24
  22.5 1.3 %collective-permute-start.6 = (bf16[128,512]{1,0:T(8,128)(2,1)S(1)}, bf16[128,512]{1,0:T(8,128)(2,1)S(1)}, u32[]{:S(2)}, u32[]{:S(2)}) collective-permute-start(bf16[128,512]{1,0:T(8,128)(2,1)S(1)} %fusion.59), channel_id=1, source_target_pairs={{0,2},{8,10},{16,18},{24,26},{1,3},{9,11},{17,19},{25,27}} | collective-permute-start | bytes 393224 | tf_op jit(solution)/shard_map/ppermute | solution.py:24
  23.8 0.7 collective-permute-start.5
  24.5 0.6 fusion.61
  25.1 1.2 %collective-permute-start.15 = (f32[512,512]{1,0:T(8,128)S(1)}, f32[512,512]{1,0:T(8,128)S(1)}, u32[]{:S(2)}, u32[]{:S(2)}) collective-permute-start(f32[512,512]{1,0:T(8,128)S(1)} %fusion.61), channel_id=1, source_target_pairs={{0,1},{1,0},{2,3},{3,2},{4,5},{5,4},{6,7},{7,6},{8,9},{9,8},{10,11... | collective-permute-start | bytes 3145736 | tf_op jit(solution)/shard_map/ppermute | solution.py:20
  26.3 2.0 %collective-permute-done.7 = bf16[128,512]{1,0:T(8,128)(2,1)S(1)} collective-permute-done((bf16[128,512]{1,0:T(8,128)(2,1)S(1)}, bf16[128,512]{1,0:T(8,128)(2,1)S(1)}, u32[]{:S(2)}, u32[]{:S(2)}) %collective-permute-start.7) | collective-permute-done | bytes 131104 | tf_op jit(solution)/shard_map/ppermute | solution.py:24
  28.5 0.7 fusion.49
  29.2 1.3 %collective-permute-start.9 = (bf16[128,512]{1,0:T(8,128)(2,1)S(1)}, bf16[128,512]{1,0:T(8,128)(2,1)S(1)}, u32[]{:S(2)}, u32[]{:S(2)}) collective-permute-start(bf16[128,512]{1,0:T(8,128)(2,1)S(1)} %fusion.49), channel_id=1, source_target_pairs={{10,6},{26,22},{11,7},{27,23}} | collective-permute-start | bytes 393224 | tf_op jit(solution)/shard_map/ppermute | solution.py:24
  30.5 0.7 collective-permute-start.8
  31.2 0.6 fusion.60
  31.8 2.0 %collective-permute-start.13 = (f32[512,512]{1,0:T(8,128)S(1)}, f32[512,512]{1,0:T(8,128)S(1)}, u32[]{:S(2)}, u32[]{:S(2)}) collective-permute-start(f32[512,512]{1,0:T(8,128)S(1)} %fusion.60), channel_id=1, source_target_pairs={{0,1},{1,0},{2,3},{3,2},{4,5},{5,4},{6,7},{7,6},{8,9},{9,8},{10,11... | collective-permute-start | bytes 3145736 | tf_op jit(solution)/shard_map/ppermute | solution.py:20
  33.9 0.7 convolution_convert_fusion
  34.6 0.7 collective-permute-start.11
  35.3 0.7 collective-permute-start.10
  36.0 0.7 convolution_subtract_fusion.5
  38.0 0.7 collective-permute-start.17
  38.7 0.7 collective-permute-start.16
  39.8 1.3 %collective-permute-start.19 = (bf16[128,512]{1,0:T(8,128)(2,1)S(1)}, bf16[128,512]{1,0:T(8,128)(2,1)S(1)}, u32[]{:S(2)}, u32[]{:S(2)}) collective-permute-start(bf16[128,512]{1,0:T(8,128)(2,1)S(1)} %fusion.19), channel_id=1, source_target_pairs={{6,10},{22,26},{7,11},{23,27}} | collective-permute-start | bytes 393224 | tf_op jit(solution)/shard_map/ppermute | solution.py:24
  41.1 0.7 collective-permute-start.18
  41.8 12.8 %collective-permute-done.19 = bf16[128,512]{1,0:T(8,128)(2,1)S(1)} collective-permute-done((bf16[128,512]{1,0:T(8,128)(2,1)S(1)}, bf16[128,512]{1,0:T(8,128)(2,1)S(1)}, u32[]{:S(2)}, u32[]{:S(2)}) %collective-permute-start.19) | collective-permute-done | bytes 131104 | tf_op jit(solution)/shard_map/ppermute | solution.py:24
  54.6 0.5 fusion.20
  55.0 1.3 %collective-permute-start.21 = (bf16[128,512]{1,0:T(8,128)(2,1)S(1)}, bf16[128,512]{1,0:T(8,128)(2,1)S(1)}, u32[]{:S(2)}, u32[]{:S(2)}) collective-permute-start(bf16[128,512]{1,0:T(8,128)(2,1)S(1)} %fusion.20), channel_id=1, source_target_pairs={{2,4},{10,12},{18,20},{26,28},{3,5},{11,13},{19,21},{27,29}} | collective-permute-start | bytes 393224 | tf_op jit(solution)/shard_map/ppermute | solution.py:24
  56.3 1.3 %collective-permute-start.20 = (bf16[128,512]{1,0:T(8,128)(2,1)S(1)}, bf16[128,512]{1,0:T(8,128)(2,1)S(1)}, u32[]{:S(2)}, u32[]{:S(2)}) collective-permute-start(bf16[128,512]{1,0:T(8,128)(2,1)S(1)} %fusion.20), channel_id=1, source_target_pairs={{2,0},{10,8},{18,16},{26,24},{3,1},{11,9},{19,17},{27,25}} | collective-permute-start | bytes 393224 | tf_op jit(solution)/shard_map/ppermute | solution.py:24
  57.6 0.7 collective-permute-start.14
  58.3 1.3 %collective-permute-done.20 = bf16[128,512]{1,0:T(8,128)(2,1)S(1)} collective-permute-done((bf16[128,512]{1,0:T(8,128)(2,1)S(1)}, bf16[128,512]{1,0:T(8,128)(2,1)S(1)}, u32[]{:S(2)}, u32[]{:S(2)}) %collective-permute-start.20) | collective-permute-done | bytes 131104 | tf_op jit(solution)/shard_map/ppermute | solution.py:24
  59.6 0.5 convolution_subtract_fusion.1
  60.2 1.3 %collective-permute-start.22 = (bf16[128,512]{1,0:T(8,128)(2,1)S(1)}, bf16[128,512]{1,0:T(8,128)(2,1)S(1)}, u32[]{:S(2)}, u32[]{:S(2)}) collective-permute-start(bf16[128,512]{1,0:T(8,128)(2,1)S(1)} %get-tuple-element.8), channel_id=1, source_target_pairs={{0,2},{4,6},{8,10},{12,14},{16,18},{20,22},{24,26},{28,30},{1,3},{... | collective-permute-start | bytes 393224 | tf_op jit(solution)/shard_map/ppermute | solution.py:108
  61.5 4.4 %collective-permute-done.22 = bf16[128,512]{1,0:T(8,128)(2,1)S(1)} collective-permute-done((bf16[128,512]{1,0:T(8,128)(2,1)S(1)}, bf16[128,512]{1,0:T(8,128)(2,1)S(1)}, u32[]{:S(2)}, u32[]{:S(2)}) %collective-permute-start.22) | collective-permute-done | bytes 131104 | tf_op jit(solution)/shard_map/ppermute | solution.py:108
  65.9 11.0 %collective-permute-start.23 = (bf16[128,512]{1,0:T(8,128)(2,1)S(1)}, bf16[128,512]{1,0:T(8,128)(2,1)S(1)}, u32[]{:S(2)}, u32[]{:S(2)}) collective-permute-start(bf16[128,512]{1,0:T(8,128)(2,1)S(1)} %broadcast_select_fusion.1), channel_id=1, source_target_pairs={{0,1},{1,0},{2,3},{3,2},{4,5},{5,4},{6,7},{7,6},{8,9},{9,8},{10,11... | collective-permute-start | bytes 393224 | tf_op jit(solution)/shard_map/ppermute | solution.py:20
  76.9 1.0 %collective-permute-done.23 = bf16[128,512]{1,0:T(8,128)(2,1)S(1)} collective-permute-done((bf16[128,512]{1,0:T(8,128)(2,1)S(1)}, bf16[128,512]{1,0:T(8,128)(2,1)S(1)}, u32[]{:S(2)}, u32[]{:S(2)}) %collective-permute-start.23) | collective-permute-done | bytes 131104 | tf_op jit(solution)/shard_map/ppermute | solution.py:20
  77.9 1.5 %fusion.14 = bf16[256,1024]{1,0:T(8,128)(2,1)S(1)} fusion(bf16[1,512,1024]{2,1,0:T(8,128)(2,1)S(1)} %copy-done, bf16[256,1024]{1,0:T(8,128)(2,1)} %copy-done.3, bf16[128,512]{1,0:T(8,128)(2,1)S(1)} %collective-permute-done.23, bf16[128,512]{1,0:T(8,128)(2,1)S(1)} %broadcast_select_fusion.1, pred[]{:T(512)S(6)} %eq.11), kind=kOutput, calls=%fused_computation.11 | convolution fusion | flops 270401536 | bytes 2359297 | tf_op jit(solution)/shard_map/dot_general | solution.py:115
  79.4 3.3 %fusion.2 = f32[256,1024]{1,0:T(8,128)} fusion(bf16[256,1024]{1,0:T(8,128)(2,1)S(1)} %fusion.14, bf16[1,1024,2048]{2,1,0:T(8,128)(2,1)} %param.7, s32[]{:T(128)S(6)} %select_n.101), kind=kOutput, calls=%fused_computation.2 | convolution fusion | flops 536870912 | bytes 3670020 | tf_op jit(solution)/shard_map/dot_general | solution.py:13
  83.3 2.5 %collective-permute-done.25 = f32[128,256]{1,0:T(8,128)S(1)} collective-permute-done((f32[128,256]{1,0:T(8,128)S(1)}, f32[128,256]{1,0:T(8,128)S(1)}, u32[]{:S(2)}, u32[]{:S(2)}) %collective-permute-start.25) | collective-permute-done | bytes 131104 | tf_op jit(solution)/shard_map/ppermute | solution.py:20
  85.7 0.7 maximum_select_fusion.5
  86.5 3.3 %fusion.11 = f32[1,256,1024]{2,1,0:T(8,128)} fusion(f32[256,1024]{1,0:T(8,128)S(1)} %collective-permute-done.24, bf16[256,1024]{1,0:T(8,128)(2,1)S(1)} %fusion.14, bf16[1,1024,2048]{2,1,0:T(8,128)(2,1)} %param.7, s32[]{:T(128)S(6)} %select_n.100), kind=kOutput, calls=%fused_computation.9 | convolution fusion | flops 537133056 | bytes 4718596 | tf_op jit(solution)/shard_map/dot_general | solution.py:13
  (43 shorter events, 3.5 us)
Async XLA Ops:
  0.6 6.8 %copy-start = (bf16[1,512,1024]{2,1,0:T(8,128)(2,1)S(1)}, bf16[1,512,1024]{2,1,0:T(8,128)(2,1)}, u32[]{:S(2)}) copy-start(bf16[1,512,1024]{2,1,0:T(8,128)(2,1)} %param.8) | copy-start | bytes 3145732
  0.6 2.8 %copy-start.5 = (bf16[1,256,1024]{2,1,0:T(8,128)(2,1)S(1)}, bf16[1,256,1024]{2,1,0:T(8,128)(2,1)}, u32[]{:S(2)}) copy-start(bf16[1,256,1024]{2,1,0:T(8,128)(2,1)} %param.6) | copy-start | bytes 1572868
  0.7 2.8 %collective-permute-start = (bf16[256,1024]{1,0:T(8,128)(2,1)}, bf16[256,1024]{1,0:T(8,128)(2,1)}, u32[]{:S(2)}, u32[]{:S(2)}) collective-permute-start(bf16[256,1024]{1,0:T(8,128)(2,1)} %bitcast.61), channel_id=1, source_target_pairs={{0,1},{1,0},{2,3},{3,2},{4,5},{5,4},{6,7},{7,6},{8,9},{9,8},{10,11... | collective-permute-start | bytes 1572872 | tf_op jit(solution)/shard_map/ppermute | solution.py:20
  3.2 4.2 %copy-start.2 = (f32[512,512]{1,0:T(8,128)}, f32[512,512]{1,0:T(8,128)S(1)}, u32[]{:S(2)}) copy-start(f32[512,512]{1,0:T(8,128)S(1)} %fusion.35) | copy-start | bytes 3145732
  3.2 15.6 %collective-permute-start.4 = (f32[512,512]{1,0:T(8,128)S(1)}, f32[512,512]{1,0:T(8,128)}, u32[]{:S(2)}, u32[]{:S(2)}) collective-permute-start(f32[512,512]{1,0:T(8,128)S(1)} %fusion.35), channel_id=1, source_target_pairs={{0,1},{1,0},{2,3},{3,2},{4,5},{5,4},{6,7},{7,6},{8,9},{9,8},{10,11... | collective-permute-start | bytes 3145736 | tf_op jit(solution)/shard_map/ppermute | solution.py:20
  3.4 5.5 %copy-start.4 = (f32[1,256,256]{2,1,0:T(8,128)S(1)}, f32[1,256,256]{2,1,0:T(8,128)}, u32[]{:S(2)}) copy-start(f32[1,256,256]{2,1,0:T(8,128)} %param.9) | copy-start | bytes 786436
  7.4 8.0 %copy-start.3 = (bf16[256,1024]{1,0:T(8,128)(2,1)}, bf16[256,1024]{1,0:T(8,128)(2,1)S(1)}, u32[]{:S(2)}) copy-start(bf16[256,1024]{1,0:T(8,128)(2,1)S(1)} %fusion.15) | copy-start | bytes 1572868
  7.4 8.0 %copy-start.1 = (f32[1,256,512]{2,1,0:T(8,128)S(1)}, f32[1,256,512]{2,1,0:T(8,128)}, u32[]{:S(2)}) copy-start(f32[1,256,512]{2,1,0:T(8,128)} %param.10) | copy-start | bytes 1572868
  8.6 1.9 %collective-permute-start.2 = (f32[128,512]{1,0:T(8,128)}, f32[128,512]{1,0:T(8,128)}, u32[]{:S(2)}, u32[]{:S(2)}) collective-permute-start(f32[128,512]{1,0:T(8,128)} %fusion.27), channel_id=1, source_target_pairs={{0,1},{1,0},{2,3},{3,2},{4,5},{5,4},{6,7},{7,6},{8,9},{9,8},{10,11... | collective-permute-start | bytes 786440 | tf_op jit(solution)/shard_map/ppermute | solution.py:20
  9.5 6.6 %collective-permute-start.1 = (f32[128,256]{1,0:T(8,128)}, f32[128,256]{1,0:T(8,128)}, u32[]{:S(2)}, u32[]{:S(2)}) collective-permute-start(f32[128,256]{1,0:T(8,128)} %get-tuple-element.14), channel_id=1, source_target_pairs={{0,1},{1,0},{2,3},{3,2},{4,5},{5,4},{6,7},{7,6},{8,9},{9,8},{10,11... | collective-permute-start | bytes 393224 | tf_op jit(solution)/shard_map/ppermute | solution.py:20
  12.6 5.1 %collective-permute-start.3 = (bf16[128,512]{1,0:T(8,128)(2,1)}, bf16[128,512]{1,0:T(8,128)(2,1)}, u32[]{:S(2)}, u32[]{:S(2)}) collective-permute-start(bf16[128,512]{1,0:T(8,128)(2,1)} %get-tuple-element.16), channel_id=1, source_target_pairs={{2,0},{6,4},{10,8},{14,12},{18,16},{22,20},{26,24},{30,28},{3,1},{... | collective-permute-start | bytes 393224 | tf_op jit(solution)/shard_map/ppermute | solution.py:24
  15.4 15.8 %collective-permute-start.12 = (f32[256,512]{1,0:T(8,128)S(1)}, f32[256,512]{1,0:T(8,128)S(1)}, u32[]{:S(2)}, u32[]{:S(2)}) collective-permute-start(f32[256,512]{1,0:T(8,128)S(1)} %bitcast.58), channel_id=1, source_target_pairs={{30,14},{31,15}} | collective-permute-start | bytes 1572872 | tf_op jit(solution)/shard_map/ppermute | solution.py:62
  21.2 7.1 %collective-permute-start.7 = (bf16[128,512]{1,0:T(8,128)(2,1)S(1)}, bf16[128,512]{1,0:T(8,128)(2,1)S(1)}, u32[]{:S(2)}, u32[]{:S(2)}) collective-permute-start(bf16[128,512]{1,0:T(8,128)(2,1)S(1)} %fusion.59), channel_id=1, source_target_pairs={{4,2},{12,10},{20,18},{28,26},{5,3},{13,11},{21,19},{29,27}} | collective-permute-start | bytes 393224 | tf_op jit(solution)/shard_map/ppermute | solution.py:24
  22.5 6.0 %collective-permute-start.6 = (bf16[128,512]{1,0:T(8,128)(2,1)S(1)}, bf16[128,512]{1,0:T(8,128)(2,1)S(1)}, u32[]{:S(2)}, u32[]{:S(2)}) collective-permute-start(bf16[128,512]{1,0:T(8,128)(2,1)S(1)} %fusion.59), channel_id=1, source_target_pairs={{0,2},{8,10},{16,18},{24,26},{1,3},{9,11},{17,19},{25,27}} | collective-permute-start | bytes 393224 | tf_op jit(solution)/shard_map/ppermute | solution.py:24
  23.8 12.1 %collective-permute-start.5 = (f32[128,512]{1,0:T(8,128)S(1)}, f32[128,512]{1,0:T(8,128)S(1)}, u32[]{:S(2)}, u32[]{:S(2)}) collective-permute-start(f32[128,512]{1,0:T(8,128)S(1)} %get-tuple-element.5), channel_id=1, source_target_pairs={{30,14},{31,15}} | collective-permute-start | bytes 786440 | tf_op jit(solution)/shard_map/ppermute | solution.py:88
  25.1 11.5 %collective-permute-start.15 = (f32[512,512]{1,0:T(8,128)S(1)}, f32[512,512]{1,0:T(8,128)S(1)}, u32[]{:S(2)}, u32[]{:S(2)}) collective-permute-start(f32[512,512]{1,0:T(8,128)S(1)} %fusion.61), channel_id=1, source_target_pairs={{0,1},{1,0},{2,3},{3,2},{4,5},{5,4},{6,7},{7,6},{8,9},{9,8},{10,11... | collective-permute-start | bytes 3145736 | tf_op jit(solution)/shard_map/ppermute | solution.py:20
  29.2 4.7 %collective-permute-start.9 = (bf16[128,512]{1,0:T(8,128)(2,1)S(1)}, bf16[128,512]{1,0:T(8,128)(2,1)S(1)}, u32[]{:S(2)}, u32[]{:S(2)}) collective-permute-start(bf16[128,512]{1,0:T(8,128)(2,1)S(1)} %fusion.49), channel_id=1, source_target_pairs={{10,6},{26,22},{11,7},{27,23}} | collective-permute-start | bytes 393224 | tf_op jit(solution)/shard_map/ppermute | solution.py:24
  30.5 3.4 %collective-permute-start.8 = (bf16[128,512]{1,0:T(8,128)(2,1)S(1)}, bf16[128,512]{1,0:T(8,128)(2,1)S(1)}, u32[]{:S(2)}, u32[]{:S(2)}) collective-permute-start(bf16[128,512]{1,0:T(8,128)(2,1)S(1)} %fusion.49), channel_id=1, source_target_pairs={{2,6},{18,22},{3,7},{19,23}} | collective-permute-start | bytes 393224 | tf_op jit(solution)/shard_map/ppermute | solution.py:24
  31.8 5.3 %collective-permute-start.13 = (f32[512,512]{1,0:T(8,128)S(1)}, f32[512,512]{1,0:T(8,128)S(1)}, u32[]{:S(2)}, u32[]{:S(2)}) collective-permute-start(f32[512,512]{1,0:T(8,128)S(1)} %fusion.60), channel_id=1, source_target_pairs={{0,1},{1,0},{2,3},{3,2},{4,5},{5,4},{6,7},{7,6},{8,9},{9,8},{10,11... | collective-permute-start | bytes 3145736 | tf_op jit(solution)/shard_map/ppermute | solution.py:20
  34.6 1.4 %collective-permute-start.11 = (bf16[128,512]{1,0:T(8,128)(2,1)S(1)}, bf16[128,512]{1,0:T(8,128)(2,1)S(1)}, u32[]{:S(2)}, u32[]{:S(2)}) collective-permute-start(bf16[128,512]{1,0:T(8,128)(2,1)S(1)} %convolution_convert_fusion), channel_id=1, source_target_pairs={{22,14},{23,15}} | collective-permute-start | bytes 393224 | tf_op jit(solution)/shard_map/ppermute | solution.py:24
  35.3 0.7 collective-permute-start.10
  38.0 1.4 %collective-permute-start.17 = (bf16[128,512]{1,0:T(8,128)(2,1)S(1)}, bf16[128,512]{1,0:T(8,128)(2,1)S(1)}, u32[]{:S(2)}, u32[]{:S(2)}) collective-permute-start(bf16[128,512]{1,0:T(8,128)(2,1)S(1)} %fusion.18), channel_id=1, source_target_pairs={{14,22},{15,23}} | collective-permute-start | bytes 393224 | tf_op jit(solution)/shard_map/ppermute | solution.py:24
  38.7 0.7 collective-permute-start.16
  39.8 14.8 %collective-permute-start.19 = (bf16[128,512]{1,0:T(8,128)(2,1)S(1)}, bf16[128,512]{1,0:T(8,128)(2,1)S(1)}, u32[]{:S(2)}, u32[]{:S(2)}) collective-permute-start(bf16[128,512]{1,0:T(8,128)(2,1)S(1)} %fusion.19), channel_id=1, source_target_pairs={{6,10},{22,26},{7,11},{23,27}} | collective-permute-start | bytes 393224 | tf_op jit(solution)/shard_map/ppermute | solution.py:24
  41.1 13.5 %collective-permute-start.18 = (bf16[128,512]{1,0:T(8,128)(2,1)S(1)}, bf16[128,512]{1,0:T(8,128)(2,1)S(1)}, u32[]{:S(2)}, u32[]{:S(2)}) collective-permute-start(bf16[128,512]{1,0:T(8,128)(2,1)S(1)} %fusion.19), channel_id=1, source_target_pairs={{6,2},{22,18},{7,3},{23,19}} | collective-permute-start | bytes 393224 | tf_op jit(solution)/shard_map/ppermute | solution.py:24
  55.0 3.3 %collective-permute-start.21 = (bf16[128,512]{1,0:T(8,128)(2,1)S(1)}, bf16[128,512]{1,0:T(8,128)(2,1)S(1)}, u32[]{:S(2)}, u32[]{:S(2)}) collective-permute-start(bf16[128,512]{1,0:T(8,128)(2,1)S(1)} %fusion.20), channel_id=1, source_target_pairs={{2,4},{10,12},{18,20},{26,28},{3,5},{11,13},{19,21},{27,29}} | collective-permute-start | bytes 393224 | tf_op jit(solution)/shard_map/ppermute | solution.py:24
  56.3 3.3 %collective-permute-start.20 = (bf16[128,512]{1,0:T(8,128)(2,1)S(1)}, bf16[128,512]{1,0:T(8,128)(2,1)S(1)}, u32[]{:S(2)}, u32[]{:S(2)}) collective-permute-start(bf16[128,512]{1,0:T(8,128)(2,1)S(1)} %fusion.20), channel_id=1, source_target_pairs={{2,0},{10,8},{18,16},{26,24},{3,1},{11,9},{19,17},{27,25}} | collective-permute-start | bytes 393224 | tf_op jit(solution)/shard_map/ppermute | solution.py:24
  57.6 2.5 %collective-permute-start.14 = (f32[128,512]{1,0:T(8,128)S(1)}, f32[128,512]{1,0:T(8,128)S(1)}, u32[]{:S(2)}, u32[]{:S(2)}) collective-permute-start(f32[128,512]{1,0:T(8,128)S(1)} %fusion.32), channel_id=1, source_target_pairs={{14,30},{15,31}} | collective-permute-start | bytes 786440 | tf_op jit(solution)/shard_map/ppermute | solution.py:105
  60.2 5.7 %collective-permute-start.22 = (bf16[128,512]{1,0:T(8,128)(2,1)S(1)}, bf16[128,512]{1,0:T(8,128)(2,1)S(1)}, u32[]{:S(2)}, u32[]{:S(2)}) collective-permute-start(bf16[128,512]{1,0:T(8,128)(2,1)S(1)} %get-tuple-element.8), channel_id=1, source_target_pairs={{0,2},{4,6},{8,10},{12,14},{16,18},{20,22},{24,26},{28,30},{1,3},{... | collective-permute-start | bytes 393224 | tf_op jit(solution)/shard_map/ppermute | solution.py:108
  65.9 12.0 %collective-permute-start.23 = (bf16[128,512]{1,0:T(8,128)(2,1)S(1)}, bf16[128,512]{1,0:T(8,128)(2,1)S(1)}, u32[]{:S(2)}, u32[]{:S(2)}) collective-permute-start(bf16[128,512]{1,0:T(8,128)(2,1)S(1)} %broadcast_select_fusion.1), channel_id=1, source_target_pairs={{0,1},{1,0},{2,3},{3,2},{4,5},{5,4},{6,7},{7,6},{8,9},{9,8},{10,11... | collective-permute-start | bytes 393224 | tf_op jit(solution)/shard_map/ppermute | solution.py:20
  82.7 3.8 %collective-permute-start.24 = (f32[256,1024]{1,0:T(8,128)}, f32[256,1024]{1,0:T(8,128)S(1)}, u32[]{:S(2)}, u32[]{:S(2)}) collective-permute-start(f32[256,1024]{1,0:T(8,128)} %fusion.2), channel_id=1, source_target_pairs={{0,1},{1,0},{2,3},{3,2},{4,5},{5,4},{6,7},{7,6},{8,9},{9,8},{10,11... | collective-permute-start | bytes 3145736 | tf_op jit(solution)/shard_map/ppermute | solution.py:20
  83.1 2.7 %collective-permute-start.25 = (f32[128,256]{1,0:T(8,128)S(1)}, f32[128,256]{1,0:T(8,128)S(1)}, u32[]{:S(2)}, u32[]{:S(2)}) collective-permute-start(f32[128,256]{1,0:T(8,128)S(1)} %get-tuple-element.13), channel_id=1, source_target_pairs={{0,1},{1,0},{2,3},{3,2},{4,5},{5,4},{6,7},{7,6},{8,9},{9,8},{10,11... | collective-permute-start | bytes 393224 | tf_op jit(solution)/shard_map/ppermute | solution.py:20

commit v4 on v1

--- a/solution.py
+++ b/solution.py
@@ -2,6 +2,7 @@
 import jax.numpy as jnp
 from jax import lax
 from jax.sharding import PartitionSpec as P
+
 
 ROWS = (((1,), (0,)), ((), ()))
 BOTH = (((1,), (1,)), ((), ()))
@@ -31,7 +32,7 @@
     )
 
 
-def local(leaf_rhs, leaf_inv, leaf_couple, sep_rhs, sep_inv, sep_couple):
+def solve(leaf_rhs, leaf_inv, leaf_couple, sep_rhs, sep_inv, sep_couple):
     count = lax.axis_size("leaf")
     depth = count.bit_length() - 1
     place = lax.axis_index("leaf")
@@ -50,24 +51,22 @@
     def other_rows(value):
         return lax.dynamic_slice_in_dim(value, (1 - core) * half, half, 0)
 
+    inv_half = sep_inv[0]
     rhs_full = join(leaf_rhs[0], swap(leaf_rhs[0]), first, 1)
-    leaf_state = lax.dot_general(
-        rhs_full, inv_rows, BOTH, preferred_element_type=jnp.float32
-    ).astype(jnp.bfloat16)
+    top_half = lax.ppermute(inv_half, "leaf", [(top, below)])
+    leaf_state = product(rhs_full, inv_rows, BOTH, None).astype(jnp.bfloat16)
     theirs = product(other_rows(leaf_state), couple_cols, BOTH, None)
     ours = product(my_rows(leaf_state), couple_cols, BOTH, None)
 
     sep_local = sep_rhs[0]
     rhs_rows = join(my_rows(sep_local), swap(other_rows(sep_local)), first, 1)
-    inv_half = sep_inv[0]
     inverse = join(inv_half, swap(inv_half), first, 0)
     couple = join(sep_couple[0], swap(sep_couple[0]), first, 1)
-    pull = product(couple, inverse, ROWS, lax.Precision.HIGHEST)
-    gram = product(inverse, inverse, FIRST, lax.Precision.HIGHEST)
+    pull = product(couple, inverse, ROWS)
+    gram = product(inverse, inverse, FIRST)
     top_rhs = lax.ppermute(rhs_rows, "leaf", [(top, below)])
-    top_half = lax.ppermute(inv_half, "leaf", [(top, below)])
     top_inverse = join(top_half, swap(top_half), first, 0)
-    top_gram = product(top_inverse, top_inverse, FIRST, lax.Precision.HIGHEST)
+    top_gram = product(top_inverse, top_inverse, FIRST)
 
     outgoing = ours + swap(theirs)
     work = rhs_rows - jnp.where(even, outgoing, 0.0)
@@ -115,7 +114,7 @@
 
 def solution(mesh):
     return jax.shard_map(
-        local,
+        solve,
         mesh=mesh,
         in_specs=(
             P("leaf", None, "sep"),

time: 91 us -> 90.3 us (level)
  matrix products: 26 us -> 23.5 us
  waiting for transfers between devices: 39.9 us -> 42.3 us
    dot_general x2 -> x1, matrix products: 7.83 us -> 4.02 us  [solve(): spread = jnp.dot(residue, inv_rows, preferred_element_type=jnp.float32)]
    ppermute x13, waiting for transfers between devices: 32.2 us -> 34.7 us  [send(): lax.ppermute(value.astype(jnp.bfloat16), 'leaf', pairs).astype(jnp.float32)]
    dot_general x15 -> x16, matrix products: 18.1 us -> 19.5 us  [product(): lax.dot_general(left, right, dims, precision=precision, preferred_element...]
  transfers between devices with their start and end apart: 26 -> 26, of which waited for: 7 -> 7; matrix products, arithmetic and copies ran while one was open for 19% -> 17% of each run, Pallas kernels for 0% -> 0%
where the time goes in v4:
time: 90.3 us; the launch traced here: 89.9 us
  waiting for transfers between devices  42.3 us (47%)
  matrix products  23.5 us (26%)
  starting transfers between devices  18 us (20%)
  other arithmetic  3.25 us (4%)
  local copies, waits for them, and re-layouts  1.76 us (2%)
  between operations  1.11 us (1%)
    ppermute x13, waiting for transfers between devices, send(): lax.ppermute(value.astype(jnp.bfloat16), 'leaf', pairs).astype(jnp.float32)  34.7 us
    dot_general x16, matrix products, product(): lax.dot_general(left, right, dims, precision=precision, preferred_element...  19.5 us
    ppermute x13, starting transfers between devices, send(): lax.ppermute(value.astype(jnp.bfloat16), 'leaf', pairs).astype(jnp.float32)  11.4 us
    ppermute x9, waiting for transfers between devices, swap(): return lax.ppermute(value, 'sep', pairs)  5.1 us
    dot_general x1, matrix products, solve(): spread = jnp.dot(residue, inv_rows, preferred_element_type=jnp.float32)  4.02 us
    ppermute x1, waiting for transfers between devices, solve(): lax.ppermute(solved.astype(jnp.bfloat16), 'leaf', [(k, k + 1) for k in ra...  2.5 us
    ppermute x9, starting transfers between devices, swap(): return lax.ppermute(value, 'sep', pairs)  2.36 us
    broadcast_in_dim x1, other arithmetic, solve(): return (leaf_solution[None], sep_solution[None])  2.33 us
  transfers between devices with their start and end apart: 26, of which 7 were waited for; matrix products, arithmetic and copies ran while one was open for 17% of the time, Pallas kernels for 0%

profile of v4, /device:TPU:0, one launch (start us, length us, event | category | flops | bytes accessed | tf_op | source)
XLA Modules:
  0.0 89.9 jit_solution(14760591324977287760)
XLA Ops:
  0.6 0.6 collective-permute-start
  1.2 1.7 %collective-permute-done = bf16[256,1024]{1,0:T(8,128)(2,1)S(1)} collective-permute-done((bf16[256,1024]{1,0:T(8,128)(2,1)}, bf16[256,1024]{1,0:T(8,128)(2,1)S(1)}, u32[]{:S(2)}, u32[]{:S(2)}) %collective-permute-start) | collective-permute-done | bytes 524320 | tf_op jit(solution)/shard_map/ppermute | solution.py:20
  3.0 3.8 %fusion.5 = bf16[256,1024]{1,0:T(8,128)(2,1)S(1)} fusion(bf16[1,1024,2048]{2,1,0:T(8,128)(2,1)} %param.7, bf16[256,1024]{1,0:T(8,128)(2,1)S(1)} %collective-permute-done, bf16[256,1024]{1,0:T(8,128)(2,1)} %bitcast.45, pred[]{:T(512)S(6)} %eq.11), kind=kOutput, calls=%fused_computation.6 | convolution fusion | flops 1078722560 | bytes 5767169 | tf_op jit(solution)/shard_map/dot_general | solution.py:13
  6.8 0.5 fusion.29
  7.3 0.4 collective-permute-start.2
  7.9 0.4 collective-permute-start.4
  8.2 1.5 %collective-permute-start.13 = (f32[256,512]{1,0:T(8,128)}, f32[256,512]{1,0:T(8,128)}, u32[]{:S(2)}, u32[]{:S(2)}) collective-permute-start(f32[256,512]{1,0:T(8,128)} %bitcast.6), channel_id=1, source_target_pairs={{30,14},{31,15}} | collective-permute-start | bytes 1572872 | tf_op jit(solution)/shard_map/ppermute | solution.py:56
  9.9 0.5 fusion.69
  10.4 1.3 %collective-permute-start.3 = (bf16[128,512]{1,0:T(8,128)(2,1)S(1)}, bf16[128,512]{1,0:T(8,128)(2,1)S(1)}, u32[]{:S(2)}, u32[]{:S(2)}) collective-permute-start(bf16[128,512]{1,0:T(8,128)(2,1)S(1)} %get-tuple-element.10), channel_id=1, source_target_pairs={{2,0},{6,4},{10,8},{14,12},{18,16},{22,20},{26,24},{30,28},{3,1},{... | collective-permute-start | bytes 393224 | tf_op jit(solution)/shard_map/ppermute | solution.py:24
  11.7 2.9 %fusion.16 = f32[512,512]{1,0:T(8,128)S(1)} fusion(f32[512,256]{1,0:T(8,128)} %collective-permute-done.4, f32[512,256]{1,0:T(8,128)S(1)} %bitcast.47, f32[256,512]{1,0:T(8,128)} %collective-permute-done.5, f32[256,512]{1,0:T(8,128)} %bitcast.6, pred[]{:T(512)S(6)} %eq.11), kind=kOutput, calls=%fused_computation.25 | convolution fusion | flops 806879232 | bytes 3145729 | tf_op jit(solution)/shard_map/dot_general | solution.py:13
  14.6 3.7 %collective-permute-done.3 = bf16[128,512]{1,0:T(8,128)(2,1)S(1)} collective-permute-done((bf16[128,512]{1,0:T(8,128)(2,1)S(1)}, bf16[128,512]{1,0:T(8,128)(2,1)S(1)}, u32[]{:S(2)}, u32[]{:S(2)}) %collective-permute-start.3) | collective-permute-done | bytes 131104 | tf_op jit(solution)/shard_map/ppermute | solution.py:24
  18.4 0.7 convolution_convert_fusion.2
  19.1 0.7 collective-permute-start.7
  19.7 2.1 %collective-permute-start.6 = (bf16[128,512]{1,0:T(8,128)(2,1)S(1)}, bf16[128,512]{1,0:T(8,128)(2,1)S(1)}, u32[]{:S(2)}, u32[]{:S(2)}) collective-permute-start(bf16[128,512]{1,0:T(8,128)(2,1)S(1)} %convolution_convert_fusion.2), channel_id=1, source_target_pairs={{0,2},{8,10},{16,18},{24,26},{1,3},{9,11},{17,19},{25,27}} | collective-permute-start | bytes 393224 | tf_op jit(solution)/shard_map/ppermute | solution.py:24
  21.9 2.5 %collective-permute-done.6 = bf16[128,512]{1,0:T(8,128)(2,1)S(1)} collective-permute-done((bf16[128,512]{1,0:T(8,128)(2,1)S(1)}, bf16[128,512]{1,0:T(8,128)(2,1)S(1)}, u32[]{:S(2)}, u32[]{:S(2)}) %collective-permute-start.6) | collective-permute-done | bytes 131104 | tf_op jit(solution)/shard_map/ppermute | solution.py:24
  24.5 0.7 convolution_convert_fusion.1
  25.1 0.7 collective-permute-start.9
  25.8 0.7 collective-permute-start.8
  26.5 3.7 %fusion.35 = f32[512,512]{1,0:T(8,128)S(1)} fusion(f32[256,512]{1,0:T(8,128)} %collective-permute-done.5, f32[256,512]{1,0:T(8,128)} %bitcast.6, pred[]{:T(512)S(6)} %eq.11), kind=kOutput, calls=%fused_computation.45 | convolution fusion | flops 806092800 | bytes 2097153 | tf_op jit(solution)/shard_map/dot_general | solution.py:13
  30.2 0.7 collective-permute-start.12
  30.9 0.7 convolution_convert_fusion
  31.6 0.7 collective-permute-start.11
  32.3 0.7 collective-permute-start.10
  33.0 2.8 %fusion.22 = f32[512,512]{1,0:T(8,128)S(1)} fusion(f32[256,512]{1,0:T(8,128)S(1)} %collective-permute-done.14, f32[256,512]{1,0:T(8,128)} %collective-permute-done.13, pred[]{:T(512)S(6)} %eq.11), kind=kOutput, calls=%fused_computation.33 | convolution fusion | flops 806092800 | bytes 2097153 | tf_op jit(solution)/shard_map/dot_general | solution.py:13
  35.8 0.7 fusion.59
  36.5 0.5 fusion.60
  37.0 0.5 fusion.53
  37.5 0.4 fusion.8
  37.9 0.7 collective-permute-start.16
  38.5 0.7 collective-permute-start.15
  39.2 0.4 fusion.9
  39.7 0.7 collective-permute-start.18
  40.4 0.7 collective-permute-start.17
  41.1 0.5 fusion.10
  41.5 0.7 collective-permute-start.20
  42.2 1.3 %collective-permute-start.19 = (bf16[128,512]{1,0:T(8,128)(2,1)S(1)}, bf16[128,512]{1,0:T(8,128)(2,1)S(1)}, u32[]{:S(2)}, u32[]{:S(2)}) collective-permute-start(bf16[128,512]{1,0:T(8,128)(2,1)S(1)} %fusion.10), channel_id=1, source_target_pairs={{2,0},{10,8},{18,16},{26,24},{3,1},{11,9},{19,17},{27,25}} | collective-permute-start | bytes 393224 | tf_op jit(solution)/shard_map/ppermute | solution.py:24
  43.5 0.7 collective-permute-start.24
  44.2 28.4 %collective-permute-done.19 = bf16[128,512]{1,0:T(8,128)(2,1)S(1)} collective-permute-done((bf16[128,512]{1,0:T(8,128)(2,1)S(1)}, bf16[128,512]{1,0:T(8,128)(2,1)S(1)}, u32[]{:S(2)}, u32[]{:S(2)}) %collective-permute-start.19) | collective-permute-done | bytes 131104 | tf_op jit(solution)/shard_map/ppermute | solution.py:24
  72.6 0.5 convolution_subtract_fusion.1
  73.1 1.5 %collective-permute-start.21 = (bf16[128,512]{1,0:T(8,128)(2,1)S(1)}, bf16[128,512]{1,0:T(8,128)(2,1)S(1)}, u32[]{:S(2)}, u32[]{:S(2)}) collective-permute-start(bf16[128,512]{1,0:T(8,128)(2,1)S(1)} %get-tuple-element.7), channel_id=1, source_target_pairs={{0,2},{4,6},{8,10},{12,14},{16,18},{20,22},{24,26},{28,30},{1,3},{... | collective-permute-start | bytes 393224 | tf_op jit(solution)/shard_map/ppermute | solution.py:93
  74.6 2.5 %collective-permute-done.21 = bf16[128,512]{1,0:T(8,128)(2,1)S(1)} collective-permute-done((bf16[128,512]{1,0:T(8,128)(2,1)S(1)}, bf16[128,512]{1,0:T(8,128)(2,1)S(1)}, u32[]{:S(2)}, u32[]{:S(2)}) %collective-permute-start.21) | collective-permute-done | bytes 131104 | tf_op jit(solution)/shard_map/ppermute | solution.py:93
  77.2 1.5 %collective-permute-done.22 = bf16[128,512]{1,0:T(8,128)(2,1)} collective-permute-done((bf16[128,512]{1,0:T(8,128)(2,1)S(1)}, bf16[128,512]{1,0:T(8,128)(2,1)}, u32[]{:S(2)}, u32[]{:S(2)}) %collective-permute-start.22) | collective-permute-done | bytes 131104 | tf_op jit(solution)/shard_map/ppermute | solution.py:20
  78.7 4.0 %fusion = f32[256,2048]{1,0:T(8,128)S(1)} fusion(bf16[1,1024,2048]{2,1,0:T(8,128)(2,1)} %param.7, bf16[1,512,1024]{2,1,0:T(8,128)(2,1)S(1)} %copy-done, bf16[256,1024]{1,0:T(8,128)(2,1)} %copy-done.1, bf16[128,512]{1,0:T(8,128)(2,1)} %collective-permute-done.22, bf16[128,512]{1,0:T(8,128)(2,1)S(1)} %broadcast_select_fusion.1, pred[]{:T(512)S(6)} %eq.11), kind=kOutput, calls=%fused_computation | convolution fusion | flops 1344143360 | bytes 8126465 | tf_op jit(solution)/shard_map/dot_general | solution.py:101
  82.7 1.1 %constant_dynamic-slice_fusion.1 = f32[256,1024]{1,0:T(8,128)} fusion(f32[256,2048]{1,0:T(8,128)S(1)} %fusion, s32[]{:T(128)S(6)} %select_n.119), kind=kLoop, calls=%fused_computation.80 | loop fusion | bytes 2097156 | tf_op jit(solution)/shard_map/dynamic_slice | solution.py:103
  83.9 0.7 dynamic-slice_bitcast_fusion
  84.9 1.9 %collective-permute-done.25 = f32[128,256]{1,0:T(8,128)S(1)} collective-permute-done((f32[128,256]{1,0:T(8,128)}, f32[128,256]{1,0:T(8,128)S(1)}, u32[]{:S(2)}, u32[]{:S(2)}) %collective-permute-start.25) | collective-permute-done | bytes 131104 | tf_op jit(solution)/shard_map/ppermute | solution.py:20
  86.8 0.7 maximum_select_fusion.13
  87.5 2.3 %add_bitcast_fusion = f32[1,256,1024]{2,1,0:T(8,128)} fusion(f32[256,1024]{1,0:T(8,128)} %collective-permute-done.23, f32[256,2048]{1,0:T(8,128)S(1)} %fusion, s32[]{:T(128)S(6)} %select_n.118), kind=kLoop, calls=%fused_computation.43 | loop fusion | flops 262144 | bytes 3145732 | tf_op jit(solution)/shard_map/broadcast_in_dim | solution.py:112
  (38 shorter events, 1.3 us)
Async XLA Ops:
  0.6 6.1 %copy-start = (bf16[1,512,1024]{2,1,0:T(8,128)(2,1)S(1)}, bf16[1,512,1024]{2,1,0:T(8,128)(2,1)}, u32[]{:S(2)}) copy-start(bf16[1,512,1024]{2,1,0:T(8,128)(2,1)} %param.8) | copy-start | bytes 3145732
  0.6 2.3 %collective-permute-start = (bf16[256,1024]{1,0:T(8,128)(2,1)}, bf16[256,1024]{1,0:T(8,128)(2,1)S(1)}, u32[]{:S(2)}, u32[]{:S(2)}) collective-permute-start(bf16[256,1024]{1,0:T(8,128)(2,1)} %bitcast.44), channel_id=1, source_target_pairs={{0,1},{1,0},{2,3},{3,2},{4,5},{5,4},{6,7},{7,6},{8,9},{9,8},{10,11... | collective-permute-start | bytes 1572872 | tf_op jit(solution)/shard_map/ppermute | solution.py:20
  1.2 6.7 %copy-start.3 = (f32[1,512,256]{2,1,0:T(8,128)S(1)}, f32[1,512,256]{2,1,0:T(8,128)}, u32[]{:S(2)}) copy-start(f32[1,512,256]{2,1,0:T(8,128)} %param.11) | copy-start | bytes 1572868
  1.2 8.5 %copy-start.2 = (f32[1,256,256]{2,1,0:T(8,128)S(1)}, f32[1,256,256]{2,1,0:T(8,128)}, u32[]{:S(2)}) copy-start(f32[1,256,256]{2,1,0:T(8,128)} %param.9) | copy-start | bytes 786436
  6.8 4.9 %copy-start.1 = (bf16[256,1024]{1,0:T(8,128)(2,1)}, bf16[256,1024]{1,0:T(8,128)(2,1)S(1)}, u32[]{:S(2)}) copy-start(bf16[256,1024]{1,0:T(8,128)(2,1)S(1)} %fusion.5) | copy-start | bytes 1572868
  7.3 2.6 %collective-permute-start.2 = (f32[128,512]{1,0:T(8,128)S(1)}, f32[128,512]{1,0:T(8,128)S(1)}, u32[]{:S(2)}, u32[]{:S(2)}) collective-permute-start(f32[128,512]{1,0:T(8,128)S(1)} %fusion.29), channel_id=1, source_target_pairs={{0,1},{1,0},{2,3},{3,2},{4,5},{5,4},{6,7},{7,6},{8,9},{9,8},{10,11... | collective-permute-start | bytes 786440 | tf_op jit(solution)/shard_map/ppermute | solution.py:20
  7.7 4.0 %collective-permute-start.5 = (f32[256,512]{1,0:T(8,128)}, f32[256,512]{1,0:T(8,128)}, u32[]{:S(2)}, u32[]{:S(2)}) collective-permute-start(f32[256,512]{1,0:T(8,128)} %bitcast.6), channel_id=1, source_target_pairs={{0,1},{1,0},{2,3},{3,2},{4,5},{5,4},{6,7},{7,6},{8,9},{9,8},{10,11... | collective-permute-start | bytes 1572872 | tf_op jit(solution)/shard_map/ppermute | solution.py:20
  7.9 3.9 %collective-permute-start.4 = (f32[512,256]{1,0:T(8,128)S(1)}, f32[512,256]{1,0:T(8,128)}, u32[]{:S(2)}, u32[]{:S(2)}) collective-permute-start(f32[512,256]{1,0:T(8,128)S(1)} %bitcast.46), channel_id=1, source_target_pairs={{0,1},{1,0},{2,3},{3,2},{4,5},{5,4},{6,7},{7,6},{8,9},{9,8},{10,11... | collective-permute-start | bytes 1572872 | tf_op jit(solution)/shard_map/ppermute | solution.py:20
  8.2 13.6 %collective-permute-start.13 = (f32[256,512]{1,0:T(8,128)}, f32[256,512]{1,0:T(8,128)}, u32[]{:S(2)}, u32[]{:S(2)}) collective-permute-start(f32[256,512]{1,0:T(8,128)} %bitcast.6), channel_id=1, source_target_pairs={{30,14},{31,15}} | collective-permute-start | bytes 1572872 | tf_op jit(solution)/shard_map/ppermute | solution.py:56
  9.7 4.9 %collective-permute-start.1 = (f32[128,256]{1,0:T(8,128)S(1)}, f32[128,256]{1,0:T(8,128)S(1)}, u32[]{:S(2)}, u32[]{:S(2)}) collective-permute-start(f32[128,256]{1,0:T(8,128)S(1)} %get-tuple-element.8), channel_id=1, source_target_pairs={{0,1},{1,0},{2,3},{3,2},{4,5},{5,4},{6,7},{7,6},{8,9},{9,8},{10,11... | collective-permute-start | bytes 393224 | tf_op jit(solution)/shard_map/ppermute | solution.py:20
  10.4 7.9 %collective-permute-start.3 = (bf16[128,512]{1,0:T(8,128)(2,1)S(1)}, bf16[128,512]{1,0:T(8,128)(2,1)S(1)}, u32[]{:S(2)}, u32[]{:S(2)}) collective-permute-start(bf16[128,512]{1,0:T(8,128)(2,1)S(1)} %get-tuple-element.10), channel_id=1, source_target_pairs={{2,0},{6,4},{10,8},{14,12},{18,16},{22,20},{26,24},{30,28},{3,1},{... | collective-permute-start | bytes 393224 | tf_op jit(solution)/shard_map/ppermute | solution.py:24
  19.1 2.9 %collective-permute-start.7 = (bf16[128,512]{1,0:T(8,128)(2,1)S(1)}, bf16[128,512]{1,0:T(8,128)(2,1)S(1)}, u32[]{:S(2)}, u32[]{:S(2)}) collective-permute-start(bf16[128,512]{1,0:T(8,128)(2,1)S(1)} %convolution_convert_fusion.2), channel_id=1, source_target_pairs={{4,2},{12,10},{20,18},{28,26},{5,3},{13,11},{21,19},{29,27}} | collective-permute-start | bytes 393224 | tf_op jit(solution)/shard_map/ppermute | solution.py:24
  19.7 4.7 %collective-permute-start.6 = (bf16[128,512]{1,0:T(8,128)(2,1)S(1)}, bf16[128,512]{1,0:T(8,128)(2,1)S(1)}, u32[]{:S(2)}, u32[]{:S(2)}) collective-permute-start(bf16[128,512]{1,0:T(8,128)(2,1)S(1)} %convolution_convert_fusion.2), channel_id=1, source_target_pairs={{0,2},{8,10},{16,18},{24,26},{1,3},{9,11},{17,19},{25,27}} | collective-permute-start | bytes 393224 | tf_op jit(solution)/shard_map/ppermute | solution.py:24
  21.8 11.1 %collective-permute-start.14 = (f32[256,512]{1,0:T(8,128)}, f32[256,512]{1,0:T(8,128)S(1)}, u32[]{:S(2)}, u32[]{:S(2)}) collective-permute-start(f32[256,512]{1,0:T(8,128)} %collective-permute-done.13), channel_id=1, source_target_pairs={{0,1},{1,0},{2,3},{3,2},{4,5},{5,4},{6,7},{7,6},{8,9},{9,8},{10,11... | collective-permute-start | bytes 1572872 | tf_op jit(solution)/shard_map/ppermute | solution.py:20
  25.1 5.7 %collective-permute-start.9 = (bf16[128,512]{1,0:T(8,128)(2,1)S(1)}, bf16[128,512]{1,0:T(8,128)(2,1)S(1)}, u32[]{:S(2)}, u32[]{:S(2)}) collective-permute-start(bf16[128,512]{1,0:T(8,128)(2,1)S(1)} %convolution_convert_fusion.1), channel_id=1, source_target_pairs={{10,6},{26,22},{11,7},{27,23}} | collective-permute-start | bytes 393224 | tf_op jit(solution)/shard_map/ppermute | solution.py:24
  25.8 5.0 %collective-permute-start.8 = (bf16[128,512]{1,0:T(8,128)(2,1)S(1)}, bf16[128,512]{1,0:T(8,128)(2,1)S(1)}, u32[]{:S(2)}, u32[]{:S(2)}) collective-permute-start(bf16[128,512]{1,0:T(8,128)(2,1)S(1)} %convolution_convert_fusion.1), channel_id=1, source_target_pairs={{2,6},{18,22},{3,7},{19,23}} | collective-permute-start | bytes 393224 | tf_op jit(solution)/shard_map/ppermute | solution.py:24
  30.2 6.8 %collective-permute-start.12 = (f32[128,512]{1,0:T(8,128)S(1)}, f32[128,512]{1,0:T(8,128)S(1)}, u32[]{:S(2)}, u32[]{:S(2)}) collective-permute-start(f32[128,512]{1,0:T(8,128)S(1)} %get-tuple-element.3), channel_id=1, source_target_pairs={{30,14},{31,15}} | collective-permute-start | bytes 786440 | tf_op jit(solution)/shard_map/ppermute | solution.py:67
  31.6 4.2 %collective-permute-start.11 = (bf16[128,512]{1,0:T(8,128)(2,1)S(1)}, bf16[128,512]{1,0:T(8,128)(2,1)S(1)}, u32[]{:S(2)}, u32[]{:S(2)}) collective-permute-start(bf16[128,512]{1,0:T(8,128)(2,1)S(1)} %convolution_convert_fusion), channel_id=1, source_target_pairs={{22,14},{23,15}} | collective-permute-start | bytes 393224 | tf_op jit(solution)/shard_map/ppermute | solution.py:24
  32.3 3.5 %collective-permute-start.10 = (bf16[128,512]{1,0:T(8,128)(2,1)S(1)}, bf16[128,512]{1,0:T(8,128)(2,1)S(1)}, u32[]{:S(2)}, u32[]{:S(2)}) collective-permute-start(bf16[128,512]{1,0:T(8,128)(2,1)S(1)} %convolution_convert_fusion), channel_id=1, source_target_pairs={{6,14},{7,15}} | collective-permute-start | bytes 393224 | tf_op jit(solution)/shard_map/ppermute | solution.py:24
  37.9 1.4 %collective-permute-start.16 = (bf16[128,512]{1,0:T(8,128)(2,1)S(1)}, bf16[128,512]{1,0:T(8,128)(2,1)S(1)}, u32[]{:S(2)}, u32[]{:S(2)}) collective-permute-start(bf16[128,512]{1,0:T(8,128)(2,1)S(1)} %fusion.8), channel_id=1, source_target_pairs={{14,22},{15,23}} | collective-permute-start | bytes 393224 | tf_op jit(solution)/shard_map/ppermute | solution.py:24
  38.5 0.7 collective-permute-start.15
  39.7 1.4 %collective-permute-start.18 = (bf16[128,512]{1,0:T(8,128)(2,1)S(1)}, bf16[128,512]{1,0:T(8,128)(2,1)S(1)}, u32[]{:S(2)}, u32[]{:S(2)}) collective-permute-start(bf16[128,512]{1,0:T(8,128)(2,1)S(1)} %fusion.9), channel_id=1, source_target_pairs={{6,10},{22,26},{7,11},{23,27}} | collective-permute-start | bytes 393224 | tf_op jit(solution)/shard_map/ppermute | solution.py:24
  40.4 0.7 collective-permute-start.17
  41.5 2.7 %collective-permute-start.20 = (bf16[128,512]{1,0:T(8,128)(2,1)S(1)}, bf16[128,512]{1,0:T(8,128)(2,1)S(1)}, u32[]{:S(2)}, u32[]{:S(2)}) collective-permute-start(bf16[128,512]{1,0:T(8,128)(2,1)S(1)} %fusion.10), channel_id=1, source_target_pairs={{2,4},{10,12},{18,20},{26,28},{3,5},{11,13},{19,21},{27,29}} | collective-permute-start | bytes 393224 | tf_op jit(solution)/shard_map/ppermute | solution.py:24
  42.2 30.4 %collective-permute-start.19 = (bf16[128,512]{1,0:T(8,128)(2,1)S(1)}, bf16[128,512]{1,0:T(8,128)(2,1)S(1)}, u32[]{:S(2)}, u32[]{:S(2)}) collective-permute-start(bf16[128,512]{1,0:T(8,128)(2,1)S(1)} %fusion.10), channel_id=1, source_target_pairs={{2,0},{10,8},{18,16},{26,24},{3,1},{11,9},{19,17},{27,25}} | collective-permute-start | bytes 393224 | tf_op jit(solution)/shard_map/ppermute | solution.py:24
  43.5 29.6 %collective-permute-start.24 = (f32[128,512]{1,0:T(8,128)S(1)}, f32[128,512]{1,0:T(8,128)S(1)}, u32[]{:S(2)}, u32[]{:S(2)}) collective-permute-start(f32[128,512]{1,0:T(8,128)S(1)} %fusion.53), channel_id=1, source_target_pairs={{14,30},{15,31}} | collective-permute-start | bytes 786440 | tf_op jit(solution)/shard_map/ppermute | solution.py:107
  73.1 4.0 %collective-permute-start.21 = (bf16[128,512]{1,0:T(8,128)(2,1)S(1)}, bf16[128,512]{1,0:T(8,128)(2,1)S(1)}, u32[]{:S(2)}, u32[]{:S(2)}) collective-permute-start(bf16[128,512]{1,0:T(8,128)(2,1)S(1)} %get-tuple-element.7), channel_id=1, source_target_pairs={{0,2},{4,6},{8,10},{12,14},{16,18},{20,22},{24,26},{28,30},{1,3},{... | collective-permute-start | bytes 393224 | tf_op jit(solution)/shard_map/ppermute | solution.py:93
  77.1 1.5 %collective-permute-start.22 = (bf16[128,512]{1,0:T(8,128)(2,1)S(1)}, bf16[128,512]{1,0:T(8,128)(2,1)}, u32[]{:S(2)}, u32[]{:S(2)}) collective-permute-start(bf16[128,512]{1,0:T(8,128)(2,1)S(1)} %broadcast_select_fusion.1), channel_id=1, source_target_pairs={{0,1},{1,0},{2,3},{3,2},{4,5},{5,4},{6,7},{7,6},{8,9},{9,8},{10,11... | collective-permute-start | bytes 393224 | tf_op jit(solution)/shard_map/ppermute | solution.py:20
  83.7 3.8 %collective-permute-start.23 = (f32[256,1024]{1,0:T(8,128)}, f32[256,1024]{1,0:T(8,128)}, u32[]{:S(2)}, u32[]{:S(2)}) collective-permute-start(f32[256,1024]{1,0:T(8,128)} %constant_dynamic-slice_fusion.1), channel_id=1, source_target_pairs={{0,1},{1,0},{2,3},{3,2},{4,5},{5,4},{6,7},{7,6},{8,9},{9,8},{10,11... | collective-permute-start | bytes 3145736 | tf_op jit(solution)/shard_map/ppermute | solution.py:20
  84.6 2.2 %collective-permute-start.25 = (f32[128,256]{1,0:T(8,128)}, f32[128,256]{1,0:T(8,128)S(1)}, u32[]{:S(2)}, u32[]{:S(2)}) collective-permute-start(f32[128,256]{1,0:T(8,128)} %get-tuple-element.5), channel_id=1, source_target_pairs={{0,1},{1,0},{2,3},{3,2},{4,5},{5,4},{6,7},{7,6},{8,9},{9,8},{10,11... | collective-permute-start | bytes 393224 | tf_op jit(solution)/shard_map/ppermute | solution.py:20
